TPU v7x, 32 devices: a whole 2x2x4 slice. The times are simulated.
32 devices in a mesh: coarse: 16 (over z, y, x), fine: 2 (over core).
Axes of the slice: x: 2, y: 2, z: 4, core: 2. Of those that a mesh axis runs over, the one named last changes fastest.
Arguments:
- fine_residual: bfloat16 [1024, 32, 128], P(('coarse', 'fine')), may hold values from -6 to 6
- prolong_blocks: bfloat16 [1024, 128, 128], P(('coarse', 'fine')), may hold values from -0.5 to 0.5
- aggregate_map: int32 [1024], P(('coarse', 'fine')), may hold values from 0 to 15, as said below
- block_counts: int32 [16], P('coarse'), may hold values from 8 to 16, as said below
- neighbors: int32 [256, 4], P('coarse'), may hold values from 0 to 47, as said below
- coarse_blocks: bfloat16 [256, 4, 128, 128], P('coarse'), may hold values from -0.29882812 to 0.29882812
- diag_values: float32 [256, 128], P('coarse'), may hold values from 2 to 16
Outputs:
- correction: float32 [1024, 32, 128], P(('coarse', 'fine'))
- coarse_solution: float32 [256, 32, 128], P('coarse')
Inputs may be any that keep to these rules, and one draw needn't show every extreme that they name: `block_counts`: every owner has at least 8 live blocks (and at least 1); at least one owner has all 16 live. `aggregate_map`: A fine block names a live slot of its own owner: below block_counts of that owner. `neighbors`: column 0 names a live slot of the previous owner (0 to 15), columns 1 and 2 a slot of the same owner plus 16, column 3 a live slot of the next owner plus 2 * 16. Columns 1 and 2 may name dead slots.
All inputs are finite; a program needn't handle non-finite values.
Results may differ from a plain program's by a relative error of at most 0.0029.
Values may be sent and summed in bfloat16 or wider, within the bound.
No kernel may reach another device: no remote copies, remote signals or barrier semaphores. Data moves between devices by JAX's collectives and lax.ppermute only.
A program may use at most 64 MiB of HBM per device.

v0:
```python
import jax
import jax.numpy as jnp
from jax import lax
from jax.sharding import PartitionSpec as P

STEPS = 6


cheb_low = 0.5
cheb_high = 20.0


def with_halo(block, sides, width):
    for axis, dim in sides:
        count = lax.axis_size(axis)
        forward = [(i, i + 1) for i in range(count - 1)]
        backward = [(target, source) for source, target in forward]
        low = lax.ppermute(
            lax.slice_in_dim(block, block.shape[dim] - width, None, axis=dim), axis, forward
        )
        high = lax.ppermute(lax.slice_in_dim(block, 0, width, axis=dim), axis, backward)
        block = jnp.concatenate([low, block, high], axis=dim)
    return block


def couple_rows(gathered, blocks):
    return jnp.einsum("bjrk,bjkm->brm", gathered, blocks, preferred_element_type=jnp.float32)


def apply_operator(update, coarse_blocks, neighbors, diag_values, live_mask):
    rounded = update.astype(jnp.bfloat16)
    slots = rounded.shape[0]
    extended = with_halo(rounded, (("coarse", 0),), slots)
    coupled = couple_rows(jnp.take(extended, neighbors, axis=0), coarse_blocks)
    return live_mask[:, None, None] * (diag_values[:, None, :] * update + coupled)


def smooth_coarse(coarse_rhs, coarse_blocks, neighbors, diag_values, live_mask):
    middle = 0.5 * (cheb_high + cheb_low)
    radius = 0.5 * (cheb_high - cheb_low)
    sigma_ratio = middle / radius
    rho_prev = 1.0 / sigma_ratio
    remainder = coarse_rhs
    update = remainder / middle
    solution = update
    for sweep_index in range(STEPS - 1):
        remainder = remainder - apply_operator(
            update, coarse_blocks, neighbors, diag_values, live_mask
        )
        rho_next = 1.0 / (2.0 * sigma_ratio - rho_prev)
        update = rho_next * rho_prev * update + 2.0 * rho_next / radius * remainder
        solution = solution + update
        rho_prev = rho_next
    return solution


def body(
    fine_residual,
    prolong_blocks,
    aggregate_map,
    block_counts,
    neighbors,
    coarse_blocks,
    diag_values,
):
    slots = coarse_blocks.shape[0]
    slot_index = jnp.arange(slots, dtype=jnp.int32)
    live_mask = (slot_index < block_counts[0]).astype(jnp.float32)
    block_terms = jnp.einsum(
        "irk,imk->irm", fine_residual, prolong_blocks, preferred_element_type=jnp.float32
    )
    member = (aggregate_map[None, :] == slot_index[:, None]).astype(jnp.float32)
    partial_rhs = jnp.einsum("ci,irm->crm", member, block_terms, precision=lax.Precision.HIGHEST)
    coarse_rhs = lax.psum_scatter(partial_rhs, "fine", scatter_dimension=1, tiled=True)
    share = smooth_coarse(coarse_rhs, coarse_blocks, neighbors, diag_values, live_mask)
    solution = lax.all_gather(share, "fine", axis=1, tiled=True)
    rounded = solution.astype(jnp.bfloat16)
    chosen = jnp.take(rounded, aggregate_map, axis=0)
    correction = jnp.einsum(
        "irk,ikm->irm", chosen, prolong_blocks, preferred_element_type=jnp.float32
    )
    return (correction, solution)


def solution(mesh):
    placed = (
        P(("coarse", "fine"), None, None),
        P(("coarse", "fine"), None, None),
        P(("coarse", "fine")),
        P("coarse"),
        P("coarse", None),
        P("coarse", None, None, None),
        P("coarse", None),
    )
    return jax.shard_map(
        body,
        mesh=mesh,
        in_specs=placed,
        out_specs=(P(("coarse", "fine"), None, None), P("coarse", None, None)),
        check_vma=False,
    )
```

profile of v0, /device:TPU:7, one launch (start us, length us, event | category | flops | bytes accessed | tf_op | source)
XLA Modules:
  0.0 94.1 jit_solution(5654429395051256649)
XLA Ops:
  7.2 0.0 copy-start
  7.2 0.0 copy-start.8
  7.2 0.0 copy-start.7
  7.2 0.0 reduce-scatter.2.cloned.1.call-start
  7.2 2.1 %fusion.49 = f32[32,32,128]{2,1,0:T(8,128)S(1)} fusion(bf16[32,32,128]{2,1,0:T(8,128)(2,1)} %param.9, bf16[32,128,128]{2,1,0:T(8,128)(2,1)} %param.10), kind=kOutput, calls=%fused_computation.82 | convolution fusion | flops 33554432 | bytes 1835008 | tf_op jit(solution)/shard_map/irk,imk->irm/dot_general | solution.py:69
  9.3 2.0 %fusion = f32[16,32,128]{2,0,1:T(8,128)} fusion(f32[32,32,128]{2,1,0:T(8,128)S(1)} %fusion.49, s32[32]{0:T(128)} %param.11), kind=kOutput, calls=%fused_computation.11 | convolution fusion | flops 25166336 | bytes 786560 | tf_op jit(solution)/shard_map/ci,irm->crm/dot_general | solution.py:73
  11.3 0.0 reduce-scatter.2.cloned.1.call-update
  11.3 0.0 copy-done.8
  11.4 0.1 copy.55
  11.4 0.1 reshape.80
  11.5 0.1 copy.54
  12.3 8.8 %reduce-scatter.2.cloned.1.call-done = f32[16,16,128]{2,0,1:T(8,128)} async-done(((f32[16,32,128]{2,0,1:T(8,128)}), f32[16,16,128]{2,0,1:T(8,128)}) %reduce-scatter.2.cloned.1.call-update) | async-done | bytes 131088 | tf_op jit(solution)/shard_map/reduce_scatter | solution.py:74
  21.1 1.0 %multiply_convert_fusion = bf16[16,16,128]{2,0,1:T(8,128)(2,1)S(1)} fusion(f32[16,16,128]{2,0,1:T(8,128)} %reduce-scatter.2.cloned.1.call-done), kind=kLoop, calls=%fused_computation.59 | loop fusion | flops 65536 | bytes 196608 | tf_op jit(solution)/shard_map/convert_element_type | solution.py:31
  22.1 3.1 %collective-permute-start = (bf16[16,16,128]{2,0,1:T(8,128)(2,1)S(1)}, bf16[16,16,128]{2,0,1:T(8,128)(2,1)S(1)}, u32[]{:S(2)}, u32[]{:S(2)}) collective-permute-start(bf16[16,16,128]{2,0,1:T(8,128)(2,1)S(1)} %multiply_convert_fusion), channel_id=1, source_target_pairs={{0,2},{2,4},{4,6},{6,8},{8,10},{10,12},{12,14},{14,16},{16,18},{18... | collective-permute-start | bytes 196616 | tf_op jit(solution)/shard_map/ppermute | solution.py:18
  25.2 2.2 %collective-permute-start.1 = (bf16[16,16,128]{2,0,1:T(8,128)(2,1)S(1)}, bf16[16,16,128]{2,0,1:T(8,128)(2,1)S(1)}, u32[]{:S(2)}, u32[]{:S(2)}) collective-permute-start(bf16[16,16,128]{2,0,1:T(8,128)(2,1)S(1)} %multiply_convert_fusion), channel_id=1, source_target_pairs={{2,0},{4,2},{6,4},{8,6},{10,8},{12,10},{14,12},{16,14},{18,16},{20... | collective-permute-start | bytes 196616 | tf_op jit(solution)/shard_map/ppermute | solution.py:21
  27.4 0.1 collective-permute-done
  27.5 4.5 %collective-permute-done.1 = bf16[16,16,128]{2,0,1:T(8,128)(2,1)S(1)} collective-permute-done((bf16[16,16,128]{2,0,1:T(8,128)(2,1)S(1)}, bf16[16,16,128]{2,0,1:T(8,128)(2,1)S(1)}, u32[]{:S(2)}, u32[]{:S(2)}) %collective-permute-start.1) | collective-permute-done | bytes 65568 | tf_op jit(solution)/shard_map/ppermute | solution.py:21
  32.1 0.1 copy.56
  32.1 0.6 gather_fusion.1
  32.8 0.4 convolution_bitcast_fusion.4
  33.2 0.0 copy-done.2
  33.2 0.1 fusion.48
  33.3 1.9 %collective-permute-start.2 = (bf16[16,16,128]{2,0,1:T(8,128)(2,1)S(1)}, bf16[16,16,128]{2,0,1:T(8,128)(2,1)S(1)}, u32[]{:S(2)}, u32[]{:S(2)}) collective-permute-start(bf16[16,16,128]{2,0,1:T(8,128)(2,1)S(1)} %get-tuple-element.13), channel_id=1, source_target_pairs={{0,2},{2,4},{4,6},{6,8},{8,10},{10,12},{12,14},{14,16},{16,18},{18... | collective-permute-start | bytes 196616 | tf_op jit(solution)/shard_map/ppermute | solution.py:18
  35.2 3.4 %collective-permute-start.3 = (bf16[16,16,128]{2,0,1:T(8,128)(2,1)S(1)}, bf16[16,16,128]{2,0,1:T(8,128)(2,1)S(1)}, u32[]{:S(2)}, u32[]{:S(2)}) collective-permute-start(bf16[16,16,128]{2,0,1:T(8,128)(2,1)S(1)} %get-tuple-element.13), channel_id=1, source_target_pairs={{2,0},{4,2},{6,4},{8,6},{10,8},{12,10},{14,12},{16,14},{18,16},{20... | collective-permute-start | bytes 196616 | tf_op jit(solution)/shard_map/ppermute | solution.py:21
  38.6 0.0 collective-permute-done.2
  38.6 3.4 %collective-permute-done.3 = bf16[16,16,128]{2,0,1:T(8,128)(2,1)S(1)} collective-permute-done((bf16[16,16,128]{2,0,1:T(8,128)(2,1)S(1)}, bf16[16,16,128]{2,0,1:T(8,128)(2,1)S(1)}, u32[]{:S(2)}, u32[]{:S(2)}) %collective-permute-start.3) | collective-permute-done | bytes 65568 | tf_op jit(solution)/shard_map/ppermute | solution.py:21
  42.1 0.0 copy-start.9
  42.1 0.1 copy.60
  42.1 0.6 gather_fusion.2
  42.8 0.4 convolution_bitcast_fusion.3
  43.2 0.2 fusion.45
  43.4 1.9 %collective-permute-start.4 = (bf16[16,16,128]{2,0,1:T(8,128)(2,1)S(1)}, bf16[16,16,128]{2,0,1:T(8,128)(2,1)S(1)}, u32[]{:S(2)}, u32[]{:S(2)}) collective-permute-start(bf16[16,16,128]{2,0,1:T(8,128)(2,1)S(1)} %get-tuple-element.11), channel_id=1, source_target_pairs={{0,2},{2,4},{4,6},{6,8},{8,10},{10,12},{12,14},{14,16},{16,18},{18... | collective-permute-start | bytes 196616 | tf_op jit(solution)/shard_map/ppermute | solution.py:18
  45.3 3.4 %collective-permute-start.5 = (bf16[16,16,128]{2,0,1:T(8,128)(2,1)S(1)}, bf16[16,16,128]{2,0,1:T(8,128)(2,1)S(1)}, u32[]{:S(2)}, u32[]{:S(2)}) collective-permute-start(bf16[16,16,128]{2,0,1:T(8,128)(2,1)S(1)} %get-tuple-element.11), channel_id=1, source_target_pairs={{2,0},{4,2},{6,4},{8,6},{10,8},{12,10},{14,12},{16,14},{18,16},{20... | collective-permute-start | bytes 196616 | tf_op jit(solution)/shard_map/ppermute | solution.py:21
  48.7 0.0 collective-permute-done.4
  48.7 3.4 %collective-permute-done.5 = bf16[16,16,128]{2,0,1:T(8,128)(2,1)S(1)} collective-permute-done((bf16[16,16,128]{2,0,1:T(8,128)(2,1)S(1)}, bf16[16,16,128]{2,0,1:T(8,128)(2,1)S(1)}, u32[]{:S(2)}, u32[]{:S(2)}) %collective-permute-start.5) | collective-permute-done | bytes 65568 | tf_op jit(solution)/shard_map/ppermute | solution.py:21
  52.1 0.1 copy.64
  52.2 0.6 gather_fusion.3
  52.8 0.4 convolution_bitcast_fusion.2
  53.2 0.1 fusion.35
  53.4 2.2 %collective-permute-start.6 = (bf16[16,16,128]{2,0,1:T(8,128)(2,1)S(1)}, bf16[16,16,128]{2,0,1:T(8,128)(2,1)S(1)}, u32[]{:S(2)}, u32[]{:S(2)}) collective-permute-start(bf16[16,16,128]{2,0,1:T(8,128)(2,1)S(1)} %fusion.35), channel_id=1, source_target_pairs={{0,2},{2,4},{4,6},{6,8},{8,10},{10,12},{12,14},{14,16},{16,18},{18... | collective-permute-start | bytes 196616 | tf_op jit(solution)/shard_map/ppermute | solution.py:18
  55.6 3.1 %collective-permute-start.7 = (bf16[16,16,128]{2,0,1:T(8,128)(2,1)S(1)}, bf16[16,16,128]{2,0,1:T(8,128)(2,1)S(1)}, u32[]{:S(2)}, u32[]{:S(2)}) collective-permute-start(bf16[16,16,128]{2,0,1:T(8,128)(2,1)S(1)} %fusion.35), channel_id=1, source_target_pairs={{2,0},{4,2},{6,4},{8,6},{10,8},{12,10},{14,12},{16,14},{18,16},{20... | collective-permute-start | bytes 196616 | tf_op jit(solution)/shard_map/ppermute | solution.py:21
  58.7 0.6 compare_and_fusion.1
  59.2 0.0 collective-permute-done.6
  59.2 3.1 %collective-permute-done.7 = bf16[16,16,128]{2,0,1:T(8,128)(2,1)S(1)} collective-permute-done((bf16[16,16,128]{2,0,1:T(8,128)(2,1)S(1)}, bf16[16,16,128]{2,0,1:T(8,128)(2,1)S(1)}, u32[]{:S(2)}, u32[]{:S(2)}) %collective-permute-start.7) | collective-permute-done | bytes 65568 | tf_op jit(solution)/shard_map/ppermute | solution.py:21
  62.4 0.1 copy.68
  62.5 0.6 gather_fusion.4
  63.1 0.4 convolution_bitcast_fusion.1
  63.5 0.0 copy-done.3
  63.5 0.0 copy-start.5
  63.5 0.2 fusion.34
  63.7 2.0 %collective-permute-start.8 = (bf16[16,16,128]{2,0,1:T(8,128)(2,1)S(1)}, bf16[16,16,128]{2,0,1:T(8,128)(2,1)S(1)}, u32[]{:S(2)}, u32[]{:S(2)}) collective-permute-start(bf16[16,16,128]{2,0,1:T(8,128)(2,1)S(1)} %fusion.34), channel_id=1, source_target_pairs={{0,2},{2,4},{4,6},{6,8},{8,10},{10,12},{12,14},{14,16},{16,18},{18... | collective-permute-start | bytes 196616 | tf_op jit(solution)/shard_map/ppermute | solution.py:18
  65.8 3.2 %collective-permute-start.9 = (bf16[16,16,128]{2,0,1:T(8,128)(2,1)S(1)}, bf16[16,16,128]{2,0,1:T(8,128)(2,1)S(1)}, u32[]{:S(2)}, u32[]{:S(2)}) collective-permute-start(bf16[16,16,128]{2,0,1:T(8,128)(2,1)S(1)} %fusion.34), channel_id=1, source_target_pairs={{2,0},{4,2},{6,4},{8,6},{10,8},{12,10},{14,12},{16,14},{18,16},{20... | collective-permute-start | bytes 196616 | tf_op jit(solution)/shard_map/ppermute | solution.py:21
  69.0 0.6 pad_clamp_fusion
  69.6 0.0 collective-permute-done.8
  69.6 3.0 %collective-permute-done.9 = bf16[16,16,128]{2,0,1:T(8,128)(2,1)S(1)} collective-permute-done((bf16[16,16,128]{2,0,1:T(8,128)(2,1)S(1)}, bf16[16,16,128]{2,0,1:T(8,128)(2,1)S(1)}, u32[]{:S(2)}, u32[]{:S(2)}) %collective-permute-start.9) | collective-permute-done | bytes 65568 | tf_op jit(solution)/shard_map/ppermute | solution.py:21
  72.6 0.1 copy.72
  72.6 1.3 %gather_fusion.5 = bf16[64,16,128]{2,1,0:T(8,128)(2,1)} fusion(bf16[48,16,128]{2,1,0:T(8,128)(2,1)S(1)} %copy.72, s32[1024]{0:T(1024)S(1)} %pad_clamp_fusion.1), kind=kCustom, calls=%fused_computation.4.clone | custom fusion | bytes 524544 | tf_op jit(solution)/shard_map/jit(_take)/gather | solution.py:34
  74.0 1.5 %convolution_bitcast_fusion = f32[16,16,128]{2,1,0:T(8,128)S(1)} fusion(bf16[16,4,128,128]{3,2,1,0:T(8,128)(2,1)S(1)} %copy-done, bf16[16,4,16,128]{3,2,1,0:T(8,128)(2,1)} %bitcast.33, pred[16,4]{1,0:T(8,128)(4,1)S(1)} %copy.54), kind=kOutput, calls=%fused_computation.6 | convolution fusion | flops 33685504 | bytes 2490432 | tf_op jit(solution)/shard_map/bjrk,bjkm->brm/dot_general | solution.py:27
  75.5 0.0 copy-done.4
  75.5 0.2 fusion.19
  75.7 8.7 %all_gather.3 = f32[16,32,128]{2,0,1:T(8,128)S(1)} all-gather(f32[16,16,128]{2,0,1:T(8,128)S(1)} %fusion.19), channel_id=1, replica_groups=mesh['coarse'=16,'fine'=2] {'fine'}, dimensions={1}, use_global_device_ids=true | all-gather | bytes 393216 | tf_op jit(solution)/shard_map/all_gather | solution.py:76
  84.5 0.8 fusion.46
  85.2 0.7 gather_fusion
  86.0 1.2 %fusion.7 = f32[32,32,128]{2,1,0:T(8,128)} fusion(bf16[32,128,128]{2,1,0:T(8,128)(2,1)S(1)} %copy-done.1, bf16[32,32,128]{2,1,0:T(8,128)(2,1)S(1)} %gather_fusion, pred[32]{0:T(512)(128)(4,1)S(1)} %copy-done.10), kind=kOutput, calls=%fused_computation.18 | convolution fusion | flops 33685504 | bytes 1835040 | tf_op jit(solution)/shard_map/irk,ikm->irm/dot_general | solution.py:79
  (24 shorter events, 0.1 us)
Async XLA Ops:
  7.2 25.6 %copy-start = (bf16[16,4,128,128]{3,2,1,0:T(8,128)(2,1)S(1)}, bf16[16,4,128,128]{3,2,1,0:T(8,128)(2,1)}, u32[]{:S(2)}) copy-start(bf16[16,4,128,128]{3,2,1,0:T(8,128)(2,1)} %param.14) | copy-start | bytes 6291460
  7.2 4.2 %copy-start.8 = (s32[16,4]{0,1:T(4,128)S(1)}, s32[16,4]{0,1:T(4,128)}, u32[]{:S(2)}) copy-start(s32[16,4]{0,1:T(4,128)} %param.13) | copy-start | bytes 772
  7.2 5.1 %copy-start.7 = (f32[16,128]{1,0:T(8,128)S(1)}, f32[16,128]{1,0:T(8,128)}, u32[]{:S(2)}) copy-start(f32[16,128]{1,0:T(8,128)} %param.15) | copy-start | bytes 24580
  7.2 13.9 %reduce-scatter.2.cloned.1.call-start = ((), (), s32[]{:S(2)}) async-start(), calls=%async_computation.1 | async-start | bytes 393216 | tf_op jit(solution)/shard_map/reduce_scatter | solution.py:74
  21.1 12.1 %copy-start.2 = (f32[16,16,128]{2,0,1:T(8,128)S(1)}, f32[16,16,128]{2,0,1:T(8,128)}, u32[]{:S(2)}) copy-start(f32[16,16,128]{2,0,1:T(8,128)} %reduce-scatter.2.cloned.1.call-done) | copy-start | bytes 393220
  22.1 5.4 %collective-permute-start = (bf16[16,16,128]{2,0,1:T(8,128)(2,1)S(1)}, bf16[16,16,128]{2,0,1:T(8,128)(2,1)S(1)}, u32[]{:S(2)}, u32[]{:S(2)}) collective-permute-start(bf16[16,16,128]{2,0,1:T(8,128)(2,1)S(1)} %multiply_convert_fusion), channel_id=1, source_target_pairs={{0,2},{2,4},{4,6},{6,8},{8,10},{10,12},{12,14},{14,16},{16,18},{18... | collective-permute-start | bytes 196616 | tf_op jit(solution)/shard_map/ppermute | solution.py:18
  25.2 6.8 %collective-permute-start.1 = (bf16[16,16,128]{2,0,1:T(8,128)(2,1)S(1)}, bf16[16,16,128]{2,0,1:T(8,128)(2,1)S(1)}, u32[]{:S(2)}, u32[]{:S(2)}) collective-permute-start(bf16[16,16,128]{2,0,1:T(8,128)(2,1)S(1)} %multiply_convert_fusion), channel_id=1, source_target_pairs={{2,0},{4,2},{6,4},{8,6},{10,8},{12,10},{14,12},{16,14},{18,16},{20... | collective-permute-start | bytes 196616 | tf_op jit(solution)/shard_map/ppermute | solution.py:21
  33.3 5.3 %collective-permute-start.2 = (bf16[16,16,128]{2,0,1:T(8,128)(2,1)S(1)}, bf16[16,16,128]{2,0,1:T(8,128)(2,1)S(1)}, u32[]{:S(2)}, u32[]{:S(2)}) collective-permute-start(bf16[16,16,128]{2,0,1:T(8,128)(2,1)S(1)} %get-tuple-element.13), channel_id=1, source_target_pairs={{0,2},{2,4},{4,6},{6,8},{8,10},{10,12},{12,14},{14,16},{16,18},{18... | collective-permute-start | bytes 196616 | tf_op jit(solution)/shard_map/ppermute | solution.py:18
  35.2 6.8 %collective-permute-start.3 = (bf16[16,16,128]{2,0,1:T(8,128)(2,1)S(1)}, bf16[16,16,128]{2,0,1:T(8,128)(2,1)S(1)}, u32[]{:S(2)}, u32[]{:S(2)}) collective-permute-start(bf16[16,16,128]{2,0,1:T(8,128)(2,1)S(1)} %get-tuple-element.13), channel_id=1, source_target_pairs={{2,0},{4,2},{6,4},{8,6},{10,8},{12,10},{14,12},{16,14},{18,16},{20... | collective-permute-start | bytes 196616 | tf_op jit(solution)/shard_map/ppermute | solution.py:21
  42.1 6.6 %copy-start.9 = (s32[32]{0:T(128)S(1)}, s32[32]{0:T(128)}, u32[]{:S(2)}) copy-start(s32[32]{0:T(128)} %param.11) | copy-start | bytes 388
  43.4 5.3 %collective-permute-start.4 = (bf16[16,16,128]{2,0,1:T(8,128)(2,1)S(1)}, bf16[16,16,128]{2,0,1:T(8,128)(2,1)S(1)}, u32[]{:S(2)}, u32[]{:S(2)}) collective-permute-start(bf16[16,16,128]{2,0,1:T(8,128)(2,1)S(1)} %get-tuple-element.11), channel_id=1, source_target_pairs={{0,2},{2,4},{4,6},{6,8},{8,10},{10,12},{12,14},{14,16},{16,18},{18... | collective-permute-start | bytes 196616 | tf_op jit(solution)/shard_map/ppermute | solution.py:18
  45.3 6.8 %collective-permute-start.5 = (bf16[16,16,128]{2,0,1:T(8,128)(2,1)S(1)}, bf16[16,16,128]{2,0,1:T(8,128)(2,1)S(1)}, u32[]{:S(2)}, u32[]{:S(2)}) collective-permute-start(bf16[16,16,128]{2,0,1:T(8,128)(2,1)S(1)} %get-tuple-element.11), channel_id=1, source_target_pairs={{2,0},{4,2},{6,4},{8,6},{10,8},{12,10},{14,12},{16,14},{18,16},{20... | collective-permute-start | bytes 196616 | tf_op jit(solution)/shard_map/ppermute | solution.py:21
  53.2 10.3 %copy-start.3 = (f32[16,16,128]{2,1,0:T(8,128)}, f32[16,16,128]{2,1,0:T(8,128)S(1)}, u32[]{:S(2)}) copy-start(f32[16,16,128]{2,1,0:T(8,128)S(1)} %convolution_bitcast_fusion.2) | copy-start | bytes 393220
  53.4 5.9 %collective-permute-start.6 = (bf16[16,16,128]{2,0,1:T(8,128)(2,1)S(1)}, bf16[16,16,128]{2,0,1:T(8,128)(2,1)S(1)}, u32[]{:S(2)}, u32[]{:S(2)}) collective-permute-start(bf16[16,16,128]{2,0,1:T(8,128)(2,1)S(1)} %fusion.35), channel_id=1, source_target_pairs={{0,2},{2,4},{4,6},{6,8},{8,10},{10,12},{12,14},{14,16},{16,18},{18... | collective-permute-start | bytes 196616 | tf_op jit(solution)/shard_map/ppermute | solution.py:18
  55.6 6.8 %collective-permute-start.7 = (bf16[16,16,128]{2,0,1:T(8,128)(2,1)S(1)}, bf16[16,16,128]{2,0,1:T(8,128)(2,1)S(1)}, u32[]{:S(2)}, u32[]{:S(2)}) collective-permute-start(bf16[16,16,128]{2,0,1:T(8,128)(2,1)S(1)} %fusion.35), channel_id=1, source_target_pairs={{2,0},{4,2},{6,4},{8,6},{10,8},{12,10},{14,12},{16,14},{18,16},{20... | collective-permute-start | bytes 196616 | tf_op jit(solution)/shard_map/ppermute | solution.py:21
  63.5 10.4 %copy-start.5 = (f32[16,16,128]{2,1,0:T(8,128)}, f32[16,16,128]{2,1,0:T(8,128)S(1)}, u32[]{:S(2)}) copy-start(f32[16,16,128]{2,1,0:T(8,128)S(1)} %convolution_bitcast_fusion.1) | copy-start | bytes 393220
  63.7 5.9 %collective-permute-start.8 = (bf16[16,16,128]{2,0,1:T(8,128)(2,1)S(1)}, bf16[16,16,128]{2,0,1:T(8,128)(2,1)S(1)}, u32[]{:S(2)}, u32[]{:S(2)}) collective-permute-start(bf16[16,16,128]{2,0,1:T(8,128)(2,1)S(1)} %fusion.34), channel_id=1, source_target_pairs={{0,2},{2,4},{4,6},{6,8},{8,10},{10,12},{12,14},{14,16},{16,18},{18... | collective-permute-start | bytes 196616 | tf_op jit(solution)/shard_map/ppermute | solution.py:18
  65.8 6.8 %collective-permute-start.9 = (bf16[16,16,128]{2,0,1:T(8,128)(2,1)S(1)}, bf16[16,16,128]{2,0,1:T(8,128)(2,1)S(1)}, u32[]{:S(2)}, u32[]{:S(2)}) collective-permute-start(bf16[16,16,128]{2,0,1:T(8,128)(2,1)S(1)} %fusion.34), channel_id=1, source_target_pairs={{2,0},{4,2},{6,4},{8,6},{10,8},{12,10},{14,12},{16,14},{18,16},{20... | collective-permute-start | bytes 196616 | tf_op jit(solution)/shard_map/ppermute | solution.py:21
  74.0 1.5 %copy-start.4 = (f32[16,16,128]{2,1,0:T(8,128)S(1)}, f32[16,16,128]{2,1,0:T(8,128)}, u32[]{:S(2)}) copy-start(f32[16,16,128]{2,1,0:T(8,128)} %copy-done.3) | copy-start | bytes 393220
  74.0 1.5 %copy-start.6 = (f32[16,16,128]{2,1,0:T(8,128)S(1)}, f32[16,16,128]{2,1,0:T(8,128)}, u32[]{:S(2)}) copy-start(f32[16,16,128]{2,1,0:T(8,128)} %copy-done.5) | copy-start | bytes 393220
  74.0 12.0 %copy-start.1 = (bf16[32,128,128]{2,1,0:T(8,128)(2,1)S(1)}, bf16[32,128,128]{2,1,0:T(8,128)(2,1)}, u32[]{:S(2)}) copy-start(bf16[32,128,128]{2,1,0:T(8,128)(2,1)} %param.10) | copy-start | bytes 3145732
  75.5 10.5 %copy-start.10 = (pred[32]{0:T(512)(128)(4,1)S(1)}, pred[32]{0:T(512)(128)(4,1)}, u32[]{:S(2)}) copy-start(pred[32]{0:T(512)(128)(4,1)} %compare_and_fusion.1) | copy-start | bytes 100
Sparse Core Ops, SparseCore 0:
  11.5 9.6 reduce-scatter.1
where the time goes:
time: 94.5 us; the launch traced here: 94.1 us
  starting transfers between devices  26.5 us (28%)
  waiting for transfers between devices  26.4 us (28%)
  between operations  15.1 us (16%)
  blocking collectives  8.73 us (9%)
  matrix products  8.51 us (9%)
  local copies, waits for them, and re-layouts  5.16 us (5%)
  other arithmetic  3.8 us (4%)
    ppermute x5, waiting for transfers between devices, with_halo(): lax.ppermute(lax.slice_in_dim(block, 0, width, axis=dim), axis, backward)  17.4 us
    ppermute x5, starting transfers between devices, with_halo(): lax.ppermute(lax.slice_in_dim(block, 0, width, axis=dim), axis, backward)  15.2 us
    ppermute x5, starting transfers between devices, with_halo(): lax.ppermute(lax.slice_in_dim(block, block.shape[dim] - width, None, axis...  11.2 us
    reduce_scatter x1, waiting for transfers between devices, body(): lax.psum_scatter(partial_rhs, 'fine', scatter_dimension=1, tiled=True)  8.8 us
    all_gather x1, blocking collectives, body(): solution = lax.all_gather(share, 'fine', axis=1, tiled=True)  8.73 us
    gather x5, local copies, waits for them, and re-layouts, apply_operator(): coupled = couple_rows(jnp.take(extended, neighbors, axis=0), coarse_blocks)  3.85 us
    dot_general x5, matrix products, couple_rows(): jnp.einsum('bjrk,bjkm->brm', gathered, blocks, preferred_element_type=jnp...  3.2 us
    dot_general x1, matrix products, body(): jnp.einsum('irk,imk->irm', fine_residual, prolong_blocks, preferred_eleme...  2.08 us
  transfers between devices with their start and end apart: 11, of which 7 were waited for; matrix products, arithmetic and copies ran while one was open for 2% of the time, Pallas kernels for 0%

commit v1 on v0

v1 whole, which is shorter than its diff:
```python
import functools
import jax
import jax.numpy as jnp
from jax import lax
from jax.experimental import pallas as pl
from jax.experimental.pallas import tpu as pltpu
from jax.sharding import PartitionSpec as P

STEPS = 6
cheb_low = 0.5
cheb_high = 20.0

VMEM = pltpu.VMEM
SMEM = pltpu.SMEM
HBM = pltpu.HBM


def in_vmem(x):
    return pltpu.with_memory_space_constraint(x, VMEM)


def in_hbm(x):
    return pltpu.with_memory_space_constraint(x, HBM)


def in_smem(x):
    return pltpu.with_memory_space_constraint(x, SMEM)


def vmem_spec():
    return pl.BlockSpec(memory_space=VMEM)


def smem_spec():
    return pl.BlockSpec(memory_space=SMEM)


def params(limit):
    return pltpu.CompilerParams(vmem_limit_bytes=limit)


MIB = 1 << 20


def chebyshev_coefficients():
    middle = 0.5 * (cheb_high + cheb_low)
    radius = 0.5 * (cheb_high - cheb_low)
    sigma = middle / radius
    rho = 1.0 / sigma
    pairs = []
    for _ in range(STEPS - 1):
        rho_next = 1.0 / (2.0 * sigma - rho)
        pairs.append((rho_next * rho, 2.0 * rho_next / radius))
        rho = rho_next
    return middle, pairs


def swap_pairs(parity, owners, fine):
    pairs = []
    paired = set()
    for low in range(parity, owners - 1, 2):
        paired |= {low, low + 1}
        for k in range(fine):
            here = low * fine + k
            there = (low + 1) * fine + fine - 1 - k
            pairs += [(here, there), (there, here)]
    for owner in range(owners):
        if owner not in paired:
            pairs += [(owner * fine + k, owner * fine + fine - 1 - k) for k in range(fine)]
    return pairs


def restrict_kernel(
    chunks, fine, agg_ref, mine_ref, res_hbm, pro_hbm, pro_ref, *rest
):
    outs = rest[:fine]
    res_ref, acc_ref, sems = rest[fine:]
    blocks = pro_hbm.shape[0]
    size = blocks // chunks
    share = acc_ref.shape[2]

    def copies(c):
        part = pl.ds(c * size, size)
        return (
            pltpu.make_async_copy(pro_hbm.at[part], pro_ref.at[part], sems.at[0, c]),
            pltpu.make_async_copy(res_hbm.at[part], res_ref.at[part], sems.at[1, c]),
        )

    for c in range(chunks):
        for copy in copies(c):
            copy.start()
    acc_ref[...] = jnp.zeros_like(acc_ref)
    for c in range(chunks):
        for copy in copies(c):
            copy.wait()
        for i in range(c * size, (c + 1) * size):
            term = lax.dot_general(
                res_ref[i],
                pro_ref[i],
                (((1,), (1,)), ((), ())),
                preferred_element_type=jnp.float32,
            )
            slot = agg_ref[i]
            for s in range(fine):
                acc_ref[s, slot] += term[s * share : (s + 1) * share]
    mine = mine_ref[0]
    for m in range(fine):
        outs[m][...] = acc_ref[mine ^ m]


def own_kernel(nb_ref, w_ref, q_ref, out_ref):
    slots = q_ref.shape[0]
    for b in range(slots):
        left = jnp.concatenate(
            [q_ref[nb_ref[b, 1] - slots], q_ref[nb_ref[b, 2] - slots]], axis=1
        )
        right = jnp.concatenate([w_ref[b, 1], w_ref[b, 2]], axis=0)
        out_ref[b] = jnp.dot(left, right, preferred_element_type=jnp.float32)


def step_kernel(
    keep, scale, last, info_ref, count_ref, nb_ref, w_ref, odd_ref, even_ref, own_ref, diag_ref,
    rem_ref, upd_ref, sol_ref, *outs
):
    slots = own_ref.shape[0]
    odd_col = info_ref[1]
    even_col = info_ref[2]
    odd_ok = info_ref[3]
    even_ok = info_ref[4]
    count = count_ref[0]
    for b in range(slots):
        odd = odd_ref[nb_ref[b, odd_col] % slots]
        even = even_ref[nb_ref[b, even_col] % slots]
        odd = jnp.where(odd_ok > 0, odd, jnp.zeros_like(odd))
        even = jnp.where(even_ok > 0, even, jnp.zeros_like(even))
        left = jnp.concatenate([odd, even], axis=1)
        right = jnp.concatenate([w_ref[b, odd_col], w_ref[b, even_col]], axis=0)
        coupled = own_ref[b] + jnp.dot(left, right, preferred_element_type=jnp.float32)
        upd = upd_ref[b]
        applied = diag_ref[b : b + 1, :] * upd + coupled
        rem = rem_ref[b] - jnp.where(b < count, applied, jnp.zeros_like(applied))
        new = keep * upd + scale * rem
        sol = sol_ref[b] + new
        if last:
            outs[0][b] = sol
        else:
            outs[0][b] = rem
            outs[1][b] = new
            outs[2][b] = sol
            outs[3][b] = new.astype(outs[3].dtype)


def prolong_kernel(chunks, fine, agg_ref, mine_ref, pro_ref, *rest):
    parts = rest[:fine]
    cor_hbm, sol_ref, rounded_ref, cor_ref, sems = rest[fine:]
    share = parts[0].shape[1]
    mine = mine_ref[0]
    for s in range(fine):
        for m in range(fine):
            @pl.when((mine ^ m) == s)
            def _():
                piece = parts[m][...]
                sol_ref[:, s * share : (s + 1) * share, :] = piece
                rounded_ref[:, s * share : (s + 1) * share, :] = piece.astype(rounded_ref.dtype)
    blocks = pro_ref.shape[0]
    size = blocks // chunks

    def copy(c):
        part = pl.ds(c * size, size)
        return pltpu.make_async_copy(cor_ref.at[part], cor_hbm.at[part], sems.at[c])

    for c in range(chunks):
        for i in range(c * size, (c + 1) * size):
            cor_ref[i] = jnp.dot(
                rounded_ref[agg_ref[i]], pro_ref[i], preferred_element_type=jnp.float32
            )
        copy(c).start()
    for c in range(chunks):
        copy(c).wait()


def body(
    owners,
    fine,
    fine_residual,
    prolong_blocks,
    aggregate_map,
    block_counts,
    neighbors,
    coarse_blocks,
    diag_values,
):
    slots, _, width, _ = coarse_blocks.shape
    blocks, rhs, _ = fine_residual.shape
    share = rhs // fine
    f32 = jnp.float32
    bf16 = jnp.bfloat16
    piece = (slots, share, width)
    middle, pairs = chebyshev_coefficients()
    chunks = 4

    owner = lax.axis_index("coarse")
    k = lax.axis_index("fine")
    is_odd = owner % 2
    mine = jnp.where(is_odd == 1, fine - 1 - k, k)
    odd_ok = jnp.where(is_odd == 1, owner + 1 < owners, owner > 0)
    even_ok = jnp.where(is_odd == 1, True, owner + 1 < owners)
    info = jnp.stack(
        [
            mine,
            jnp.where(is_odd == 1, 3, 0),
            jnp.where(is_odd == 1, 0, 3),
            odd_ok.astype(jnp.int32),
            even_ok.astype(jnp.int32),
        ]
    ).astype(jnp.int32)
    info = in_smem(info)
    agg = in_smem(aggregate_map)
    count = in_smem(block_counts)
    nb = in_smem(neighbors)
    weights = in_vmem(coarse_blocks)
    diag = in_vmem(diag_values)

    pro, *sums = pl.pallas_call(
        functools.partial(restrict_kernel, chunks, fine),
        out_shape=[VMEM(prolong_blocks.shape, bf16)] + [VMEM(piece, f32)] * fine,
        in_specs=[smem_spec(), smem_spec()] + [pl.BlockSpec(memory_space=HBM)] * 2,
        out_specs=[vmem_spec()] * (fine + 1),
        scratch_shapes=[
            VMEM(fine_residual.shape, bf16),
            VMEM((fine,) + piece, f32),
            pltpu.SemaphoreType.DMA((2, chunks)),
        ],
        compiler_params=params(8 * MIB),
        name="restrict",
    )(agg, info, in_hbm(fine_residual), in_hbm(prolong_blocks))

    coarse_rhs = sums[0]
    for m in range(1, fine):
        coarse_rhs = coarse_rhs + lax.ppermute(
            sums[m], "fine", [(a, a ^ m) for a in range(fine)]
        )
    rem = coarse_rhs
    upd = coarse_rhs / middle
    sol = upd
    q = upd.astype(bf16)
    odd_pairs = swap_pairs(1, owners, fine)
    even_pairs = swap_pairs(0, owners, fine)
    for t, (keep, scale) in enumerate(pairs):
        last = t == len(pairs) - 1
        odd = lax.ppermute(q, ("coarse", "fine"), odd_pairs)
        even = lax.ppermute(q, ("coarse", "fine"), even_pairs)
        own = pl.pallas_call(
            own_kernel,
            out_shape=VMEM(piece, f32),
            in_specs=[smem_spec(), vmem_spec(), vmem_spec()],
            out_specs=vmem_spec(),
            compiler_params=params(4 * MIB),
            name="own",
        )(nb, weights, in_vmem(q))
        shapes = [VMEM(piece, f32)] if last else [VMEM(piece, f32)] * 3 + [VMEM(piece, bf16)]
        result = pl.pallas_call(
            functools.partial(step_kernel, keep, scale, last),
            out_shape=shapes,
            in_specs=[smem_spec()] * 3 + [vmem_spec()] * 8,
            out_specs=[vmem_spec()] * len(shapes),
            compiler_params=params(4 * MIB),
            name="step",
        )(
            info, count, nb, weights, in_vmem(odd), in_vmem(even), in_vmem(own), diag,
            in_vmem(rem), in_vmem(upd), in_vmem(sol),
        )
        if last:
            sol = result[0]
        else:
            rem, upd, sol, q = result

    parts = [sol] + [
        lax.ppermute(sol, "fine", [(a, a ^ m) for a in range(fine)]) for m in range(1, fine)
    ]
    correction, solution = pl.pallas_call(
        functools.partial(prolong_kernel, chunks, fine),
        out_shape=[
            HBM(fine_residual.shape, f32),
            jax.ShapeDtypeStruct((slots, rhs, width), f32),
        ],
        in_specs=[smem_spec(), smem_spec(), vmem_spec()] + [vmem_spec()] * fine,
        out_specs=[pl.BlockSpec(memory_space=HBM), vmem_spec()],
        scratch_shapes=[
            VMEM((slots, rhs, width), bf16),
            VMEM(fine_residual.shape, f32),
            pltpu.SemaphoreType.DMA((chunks,)),
        ],
        compiler_params=params(8 * MIB),
        name="prolong",
    )(agg, info, in_vmem(pro), *[in_vmem(p) for p in parts])
    return correction, solution


def solution(mesh):
    placed = (
        P(("coarse", "fine"), None, None),
        P(("coarse", "fine"), None, None),
        P(("coarse", "fine")),
        P("coarse"),
        P("coarse", None),
        P("coarse", None, None, None),
        P("coarse", None),
    )
    return jax.shard_map(
        functools.partial(body, mesh.shape["coarse"], mesh.shape["fine"]),
        mesh=mesh,
        in_specs=placed,
        out_specs=(P(("coarse", "fine"), None, None), P("coarse", None, None)),
        check_vma=False,
    )
```

time: 94.5 us -> 47.2 us (0.50)
  the two profiles are of different devices: /device:TPU:7 before, /device:TPU:9 now
where the time goes in v1:
time: 47.2 us; the launch traced here: 47 us
  waiting for transfers between devices  19.4 us (41%)
  Pallas kernels  14.4 us (31%)
  starting transfers between devices  10.1 us (21%)
  local copies, waits for them, and re-layouts  1.65 us (3%)
  between operations  1.39 us (3%)
    ppermute x5, waiting for transfers between devices, body(): odd = lax.ppermute(q, ('coarse', 'fine'), odd_pairs)  11.5 us
    ppermute x5, waiting for transfers between devices, body(): even = lax.ppermute(q, ('coarse', 'fine'), even_pairs)  5.72 us
    ppermute x5, starting transfers between devices, body(): odd = lax.ppermute(q, ('coarse', 'fine'), odd_pairs)  5.21 us
    pallas_call x5, Pallas kernels, body(): pl.pallas_call(functools.partial(step_kernel, keep, scale, last), out_sha...  4.93 us
    pallas_call x5, Pallas kernels, body(): pl.pallas_call(own_kernel, out_shape=VMEM(piece, f32), in_specs=[smem_spe...  4.54 us
    ppermute x5, starting transfers between devices, body(): even = lax.ppermute(q, ('coarse', 'fine'), even_pairs)  3.91 us
    pallas_call x1, Pallas kernels, body(): pl.pallas_call(functools.partial(restrict_kernel, chunks, fine), out_shap...  2.61 us
    pallas_call x1, Pallas kernels, body(): pl.pallas_call(functools.partial(prolong_kernel, chunks, fine), out_shape...  2.36 us
  transfers between devices with their start and end apart: 12, of which 11 were waited for; matrix products, arithmetic and copies ran while one was open for 2% of the time, Pallas kernels for 10%

profile of v1, /device:TPU:9, one launch (start us, length us, event | category | flops | bytes accessed | tf_op | source)
XLA Modules:
  0.0 47.0 jit_solution(4165472599459185808)
XLA Ops:
  0.6 0.0 copy-start
  0.7 0.1 stack.31.mine_ref.info_ref
  0.8 0.0 copy-start.4
  0.8 0.8 %copy-done.4 = s32[32]{0:T(128)S(1)} copy-done((s32[32]{0:T(128)S(1)}, s32[32]{0:T(128)}, u32[]{:S(2)}) %copy-start.4) | copy-done | bytes 152
  1.5 0.0 copy-start.2
  1.5 0.0 copy-start.1
  1.5 2.6 %restrict.1 = (bf16[32,128,128]{2,1,0:T(8,128)(2,1)S(1)}, f32[16,16,128]{2,1,0:T(8,128)S(1)}, f32[16,16,128]{2,1,0:T(8,128)S(1)}) custom-call(s32[32]{0:T(128)S(1)} %copy-done.4, s32[5]{0:T(128)S(1)} %stack.31.mine_ref.info_ref, bf16[32,32,128]{2,1,0:T(8,128)(2,1)} %res_hbm.1, bf16[32,128,128]{2,1,0:T(8,128)(2,1)} %pro_hbm.1), custom_call_target="tpu_custom_call" | custom-call | tf_op jit(solution)/shard_map/restrict/pallas_call | solution.py:224
  4.2 0.7 %collective-permute-start = (f32[16,16,128]{2,1,0:T(8,128)S(1)}, f32[16,16,128]{2,1,0:T(8,128)S(1)}, u32[]{:S(2)}, u32[]{:S(2)}) collective-permute-start(f32[16,16,128]{2,1,0:T(8,128)S(1)} %get-tuple-element.23), channel_id=1, source_target_pairs={{0,1},{1,0},{2,3},{3,2},{4,5},{5,4},{6,7},{7,6},{8,9},{9,8},{10,11... | collective-permute-start | bytes 393224 | tf_op jit(solution)/shard_map/ppermute | solution.py:240
  4.9 1.0 %collective-permute-done = f32[16,16,128]{2,1,0:T(8,128)S(1)} collective-permute-done((f32[16,16,128]{2,1,0:T(8,128)S(1)}, f32[16,16,128]{2,1,0:T(8,128)S(1)}, u32[]{:S(2)}, u32[]{:S(2)}) %collective-permute-start) | collective-permute-done | bytes 131104 | tf_op jit(solution)/shard_map/ppermute | solution.py:240
  5.9 1.5 %collective-permute-start.2 = (bf16[16,16,128]{2,1,0:T(8,128)(2,1)S(1)}, bf16[16,16,128]{2,1,0:T(8,128)(2,1)S(1)}, u32[]{:S(2)}, u32[]{:S(2)}) collective-permute-start(bf16[16,16,128]{2,1,0:T(8,128)(2,1)S(1)} %fusion.q_ref), channel_id=1, source_target_pairs={{0,3},{3,0},{1,2},{2,1},{4,7},{7,4},{5,6},{6,5},{8,11},{11,8},{9,1... | collective-permute-start | bytes 196616 | tf_op jit(solution)/shard_map/ppermute | solution.py:252
  7.5 1.1 %collective-permute-start.1 = (bf16[16,16,128]{2,1,0:T(8,128)(2,1)S(1)}, bf16[16,16,128]{2,1,0:T(8,128)(2,1)}, u32[]{:S(2)}, u32[]{:S(2)}) collective-permute-start(bf16[16,16,128]{2,1,0:T(8,128)(2,1)S(1)} %fusion.q_ref), channel_id=1, source_target_pairs={{2,5},{5,2},{3,4},{4,3},{6,9},{9,6},{7,8},{8,7},{10,13},{13,10},{1... | collective-permute-start | bytes 196616 | tf_op jit(solution)/shard_map/ppermute | solution.py:251
  8.6 0.0 copy-done.2
  9.2 0.8 %copy.18.nb_ref = s32[16,4]{1,0:T(8,128)S(1)} copy(s32[16,4]{0,1:T(4,128)} %param.11) | data formatting | bytes 512 | tf_op args[4]
  10.0 0.0 copy-done
  10.0 0.0 copy-start.3
  10.0 0.9 %own.5.own_ref = f32[16,16,128]{2,1,0:T(8,128)S(1)} custom-call(s32[16,4]{1,0:T(8,128)S(1)} %copy.18.nb_ref, bf16[16,4,128,128]{3,2,1,0:T(8,128)(2,1)S(1)} %copy-done, bf16[16,16,128]{2,1,0:T(8,128)(2,1)S(1)} %fusion.q_ref), custom_call_target="tpu_custom_call" | custom-call | tf_op jit(solution)/shard_map/own/pallas_call | solution.py:253
  10.9 0.0 collective-permute-done.2.even_ref
  10.9 2.3 %collective-permute-done.1.odd_ref = bf16[16,16,128]{2,1,0:T(8,128)(2,1)} collective-permute-done((bf16[16,16,128]{2,1,0:T(8,128)(2,1)S(1)}, bf16[16,16,128]{2,1,0:T(8,128)(2,1)}, u32[]{:S(2)}, u32[]{:S(2)}) %collective-permute-start.1) | collective-permute-done | bytes 65568 | tf_op jit(solution)/shard_map/ppermute | solution.py:251
  13.2 0.0 copy-done.1
  13.2 0.0 copy-done.3
  13.2 1.1 %step.5 = (f32[16,16,128]{2,1,0:T(8,128)S(1)}, f32[16,16,128]{2,1,0:T(8,128)S(1)}, f32[16,16,128]{2,1,0:T(8,128)S(1)}, bf16[16,16,128]{2,1,0:T(8,128)(2,1)S(1)}) custom-call(s32[5]{0:T(128)S(1)} %copy-done.3, s32[1]{0:T(128)S(6)} %copy.19.count_ref, s32[16,4]{1,0:T(8,128)S(1)} %copy.18.nb_ref, bf16[16,4,128,128]{3,2,1,0:T(8,128)(2,1)S(1)} %copy-done, ...), custom_call_target="tpu_custom_call" | custom-call | tf_op jit(solution)/shard_map/step/pallas_call | solution.py:262
  14.4 0.8 %collective-permute-start.4 = (bf16[16,16,128]{2,1,0:T(8,128)(2,1)S(1)}, bf16[16,16,128]{2,1,0:T(8,128)(2,1)S(1)}, u32[]{:S(2)}, u32[]{:S(2)}) collective-permute-start(bf16[16,16,128]{2,1,0:T(8,128)(2,1)S(1)} %get-tuple-element.24.q_ref), channel_id=1, source_target_pairs={{0,3},{3,0},{1,2},{2,1},{4,7},{7,4},{5,6},{6,5},{8,11},{11,8},{9,1... | collective-permute-start | bytes 196616 | tf_op jit(solution)/shard_map/ppermute | solution.py:252
  15.2 0.9 %collective-permute-start.3 = (bf16[16,16,128]{2,1,0:T(8,128)(2,1)S(1)}, bf16[16,16,128]{2,1,0:T(8,128)(2,1)S(1)}, u32[]{:S(2)}, u32[]{:S(2)}) collective-permute-start(bf16[16,16,128]{2,1,0:T(8,128)(2,1)S(1)} %get-tuple-element.24.q_ref), channel_id=1, source_target_pairs={{2,5},{5,2},{3,4},{4,3},{6,9},{9,6},{7,8},{8,7},{10,13},{13,10},{1... | collective-permute-start | bytes 196616 | tf_op jit(solution)/shard_map/ppermute | solution.py:251
  16.1 0.9 %own.6.own_ref = f32[16,16,128]{2,1,0:T(8,128)S(1)} custom-call(s32[16,4]{1,0:T(8,128)S(1)} %copy.18.nb_ref, bf16[16,4,128,128]{3,2,1,0:T(8,128)(2,1)S(1)} %copy-done, bf16[16,16,128]{2,1,0:T(8,128)(2,1)S(1)} %get-tuple-element.24.q_ref), custom_call_target="tpu_custom_call" | custom-call | tf_op jit(solution)/shard_map/own/pallas_call | solution.py:253
  17.0 1.3 %collective-permute-done.4.even_ref = bf16[16,16,128]{2,1,0:T(8,128)(2,1)S(1)} collective-permute-done((bf16[16,16,128]{2,1,0:T(8,128)(2,1)S(1)}, bf16[16,16,128]{2,1,0:T(8,128)(2,1)S(1)}, u32[]{:S(2)}, u32[]{:S(2)}) %collective-permute-start.4) | collective-permute-done | bytes 65568 | tf_op jit(solution)/shard_map/ppermute | solution.py:252
  18.3 2.6 %collective-permute-done.3.odd_ref = bf16[16,16,128]{2,1,0:T(8,128)(2,1)S(1)} collective-permute-done((bf16[16,16,128]{2,1,0:T(8,128)(2,1)S(1)}, bf16[16,16,128]{2,1,0:T(8,128)(2,1)S(1)}, u32[]{:S(2)}, u32[]{:S(2)}) %collective-permute-start.3) | collective-permute-done | bytes 65568 | tf_op jit(solution)/shard_map/ppermute | solution.py:251
  20.8 0.9 %step.6 = (f32[16,16,128]{2,1,0:T(8,128)S(1)}, f32[16,16,128]{2,1,0:T(8,128)S(1)}, f32[16,16,128]{2,1,0:T(8,128)S(1)}, bf16[16,16,128]{2,1,0:T(8,128)(2,1)S(1)}) custom-call(s32[5]{0:T(128)S(1)} %copy-done.3, s32[1]{0:T(128)S(6)} %copy.19.count_ref, s32[16,4]{1,0:T(8,128)S(1)} %copy.18.nb_ref, bf16[16,4,128,128]{3,2,1,0:T(8,128)(2,1)S(1)} %copy-done, ...), custom_call_target="tpu_custom_call" | custom-call | tf_op jit(solution)/shard_map/step/pallas_call | solution.py:262
  21.8 0.4 collective-permute-start.6
  22.2 1.1 %collective-permute-start.5 = (bf16[16,16,128]{2,1,0:T(8,128)(2,1)S(1)}, bf16[16,16,128]{2,1,0:T(8,128)(2,1)S(1)}, u32[]{:S(2)}, u32[]{:S(2)}) collective-permute-start(bf16[16,16,128]{2,1,0:T(8,128)(2,1)S(1)} %get-tuple-element.28.q_ref), channel_id=1, source_target_pairs={{2,5},{5,2},{3,4},{4,3},{6,9},{9,6},{7,8},{8,7},{10,13},{13,10},{1... | collective-permute-start | bytes 196616 | tf_op jit(solution)/shard_map/ppermute | solution.py:251
  23.3 0.9 %own.7.own_ref = f32[16,16,128]{2,1,0:T(8,128)S(1)} custom-call(s32[16,4]{1,0:T(8,128)S(1)} %copy.18.nb_ref, bf16[16,4,128,128]{3,2,1,0:T(8,128)(2,1)S(1)} %copy-done, bf16[16,16,128]{2,1,0:T(8,128)(2,1)S(1)} %get-tuple-element.28.q_ref), custom_call_target="tpu_custom_call" | custom-call | tf_op jit(solution)/shard_map/own/pallas_call | solution.py:253
  24.2 1.7 %collective-permute-done.6.even_ref = bf16[16,16,128]{2,1,0:T(8,128)(2,1)S(1)} collective-permute-done((bf16[16,16,128]{2,1,0:T(8,128)(2,1)S(1)}, bf16[16,16,128]{2,1,0:T(8,128)(2,1)S(1)}, u32[]{:S(2)}, u32[]{:S(2)}) %collective-permute-start.6) | collective-permute-done | bytes 65568 | tf_op jit(solution)/shard_map/ppermute | solution.py:252
  25.9 1.9 %collective-permute-done.5.odd_ref = bf16[16,16,128]{2,1,0:T(8,128)(2,1)S(1)} collective-permute-done((bf16[16,16,128]{2,1,0:T(8,128)(2,1)S(1)}, bf16[16,16,128]{2,1,0:T(8,128)(2,1)S(1)}, u32[]{:S(2)}, u32[]{:S(2)}) %collective-permute-start.5) | collective-permute-done | bytes 65568 | tf_op jit(solution)/shard_map/ppermute | solution.py:251
  27.8 0.9 %step.7 = (f32[16,16,128]{2,1,0:T(8,128)S(1)}, f32[16,16,128]{2,1,0:T(8,128)S(1)}, f32[16,16,128]{2,1,0:T(8,128)S(1)}, bf16[16,16,128]{2,1,0:T(8,128)(2,1)S(1)}) custom-call(s32[5]{0:T(128)S(1)} %copy-done.3, s32[1]{0:T(128)S(6)} %copy.19.count_ref, s32[16,4]{1,0:T(8,128)S(1)} %copy.18.nb_ref, bf16[16,4,128,128]{3,2,1,0:T(8,128)(2,1)S(1)} %copy-done, ...), custom_call_target="tpu_custom_call" | custom-call | tf_op jit(solution)/shard_map/step/pallas_call | solution.py:262
  28.8 0.8 %collective-permute-start.8 = (bf16[16,16,128]{2,1,0:T(8,128)(2,1)S(1)}, bf16[16,16,128]{2,1,0:T(8,128)(2,1)S(1)}, u32[]{:S(2)}, u32[]{:S(2)}) collective-permute-start(bf16[16,16,128]{2,1,0:T(8,128)(2,1)S(1)} %get-tuple-element.32.q_ref), channel_id=1, source_target_pairs={{0,3},{3,0},{1,2},{2,1},{4,7},{7,4},{5,6},{6,5},{8,11},{11,8},{9,1... | collective-permute-start | bytes 196616 | tf_op jit(solution)/shard_map/ppermute | solution.py:252
  29.6 0.9 %collective-permute-start.7 = (bf16[16,16,128]{2,1,0:T(8,128)(2,1)S(1)}, bf16[16,16,128]{2,1,0:T(8,128)(2,1)S(1)}, u32[]{:S(2)}, u32[]{:S(2)}) collective-permute-start(bf16[16,16,128]{2,1,0:T(8,128)(2,1)S(1)} %get-tuple-element.32.q_ref), channel_id=1, source_target_pairs={{2,5},{5,2},{3,4},{4,3},{6,9},{9,6},{7,8},{8,7},{10,13},{13,10},{1... | collective-permute-start | bytes 196616 | tf_op jit(solution)/shard_map/ppermute | solution.py:251
  30.5 0.9 %own.8.own_ref = f32[16,16,128]{2,1,0:T(8,128)S(1)} custom-call(s32[16,4]{1,0:T(8,128)S(1)} %copy.18.nb_ref, bf16[16,4,128,128]{3,2,1,0:T(8,128)(2,1)S(1)} %copy-done, bf16[16,16,128]{2,1,0:T(8,128)(2,1)S(1)} %get-tuple-element.32.q_ref), custom_call_target="tpu_custom_call" | custom-call | tf_op jit(solution)/shard_map/own/pallas_call | solution.py:253
  31.4 1.3 %collective-permute-done.8.even_ref = bf16[16,16,128]{2,1,0:T(8,128)(2,1)S(1)} collective-permute-done((bf16[16,16,128]{2,1,0:T(8,128)(2,1)S(1)}, bf16[16,16,128]{2,1,0:T(8,128)(2,1)S(1)}, u32[]{:S(2)}, u32[]{:S(2)}) %collective-permute-start.8) | collective-permute-done | bytes 65568 | tf_op jit(solution)/shard_map/ppermute | solution.py:252
  32.7 2.6 %collective-permute-done.7.odd_ref = bf16[16,16,128]{2,1,0:T(8,128)(2,1)S(1)} collective-permute-done((bf16[16,16,128]{2,1,0:T(8,128)(2,1)S(1)}, bf16[16,16,128]{2,1,0:T(8,128)(2,1)S(1)}, u32[]{:S(2)}, u32[]{:S(2)}) %collective-permute-start.7) | collective-permute-done | bytes 65568 | tf_op jit(solution)/shard_map/ppermute | solution.py:251
  35.2 0.9 %step.8 = (f32[16,16,128]{2,1,0:T(8,128)S(1)}, f32[16,16,128]{2,1,0:T(8,128)S(1)}, f32[16,16,128]{2,1,0:T(8,128)S(1)}, bf16[16,16,128]{2,1,0:T(8,128)(2,1)S(1)}) custom-call(s32[5]{0:T(128)S(1)} %copy-done.3, s32[1]{0:T(128)S(6)} %copy.19.count_ref, s32[16,4]{1,0:T(8,128)S(1)} %copy.18.nb_ref, bf16[16,4,128,128]{3,2,1,0:T(8,128)(2,1)S(1)} %copy-done, ...), custom_call_target="tpu_custom_call" | custom-call | tf_op jit(solution)/shard_map/step/pallas_call | solution.py:262
  36.2 0.0 copy-start.5
  36.2 0.4 collective-permute-start.10
  36.6 1.1 %collective-permute-start.9 = (bf16[16,16,128]{2,1,0:T(8,128)(2,1)S(1)}, bf16[16,16,128]{2,1,0:T(8,128)(2,1)S(1)}, u32[]{:S(2)}, u32[]{:S(2)}) collective-permute-start(bf16[16,16,128]{2,1,0:T(8,128)(2,1)S(1)} %get-tuple-element.36.q_ref), channel_id=1, source_target_pairs={{2,5},{5,2},{3,4},{4,3},{6,9},{9,6},{7,8},{8,7},{10,13},{13,10},{1... | collective-permute-start | bytes 196616 | tf_op jit(solution)/shard_map/ppermute | solution.py:251
  37.7 0.9 %own.9.own_ref = f32[16,16,128]{2,1,0:T(8,128)S(1)} custom-call(s32[16,4]{1,0:T(8,128)S(1)} %copy.18.nb_ref, bf16[16,4,128,128]{3,2,1,0:T(8,128)(2,1)S(1)} %copy-done, bf16[16,16,128]{2,1,0:T(8,128)(2,1)S(1)} %get-tuple-element.36.q_ref), custom_call_target="tpu_custom_call" | custom-call | tf_op jit(solution)/shard_map/own/pallas_call | solution.py:253
  38.6 1.5 %collective-permute-done.10.even_ref = bf16[16,16,128]{2,1,0:T(8,128)(2,1)S(1)} collective-permute-done((bf16[16,16,128]{2,1,0:T(8,128)(2,1)S(1)}, bf16[16,16,128]{2,1,0:T(8,128)(2,1)S(1)}, u32[]{:S(2)}, u32[]{:S(2)}) %collective-permute-start.10) | collective-permute-done | bytes 65568 | tf_op jit(solution)/shard_map/ppermute | solution.py:252
  40.1 2.1 %collective-permute-done.9.odd_ref = bf16[16,16,128]{2,1,0:T(8,128)(2,1)S(1)} collective-permute-done((bf16[16,16,128]{2,1,0:T(8,128)(2,1)S(1)}, bf16[16,16,128]{2,1,0:T(8,128)(2,1)S(1)}, u32[]{:S(2)}, u32[]{:S(2)}) %collective-permute-start.9) | collective-permute-done | bytes 65568 | tf_op jit(solution)/shard_map/ppermute | solution.py:251
  42.2 0.9 %step.9.rest_0_ = f32[16,16,128]{2,1,0:T(8,128)S(1)} custom-call(s32[5]{0:T(128)S(1)} %copy-done.3, s32[1]{0:T(128)S(6)} %copy.19.count_ref, s32[16,4]{1,0:T(8,128)S(1)} %copy.18.nb_ref, bf16[16,4,128,128]{3,2,1,0:T(8,128)(2,1)S(1)} %copy-done, bf16[16,16,128]{2,1,0:T(8,128)(2,1)S(1)} %collective-permute-done.9.odd_ref, ...), custom_call_target="tpu_custom_call" | custom-call | tf_op jit(solution)/shard_map/step/pallas_call | solution.py:262
  43.2 0.2 collective-permute-start.11
  43.4 1.2 %collective-permute-done.11.rest_1_ = f32[16,16,128]{2,1,0:T(8,128)S(1)} collective-permute-done((f32[16,16,128]{2,1,0:T(8,128)S(1)}, f32[16,16,128]{2,1,0:T(8,128)S(1)}, u32[]{:S(2)}, u32[]{:S(2)}) %collective-permute-start.11) | collective-permute-done | bytes 131104 | tf_op jit(solution)/shard_map/ppermute | solution.py:279
  44.6 0.0 copy-done.5
  44.6 2.4 %prolong.1 = (f32[32,32,128]{2,1,0:T(8,128)}, f32[16,32,128]{2,1,0:T(8,128)}) custom-call(s32[32]{0:T(128)S(1)} %copy-done.5, s32[5]{0:T(128)S(1)} %copy-done.3, bf16[32,128,128]{2,1,0:T(8,128)(2,1)S(1)} %get-tuple-element.21.pro_ref, f32[16,16,128]{2,1,0:T(8,128)S(1)} %step.9.rest_0_, f32[16,16,128]{2,1,0:T(8,128)S(1)} %collective-permute-done.11.rest_1_), custom_call_target="tpu_custom_call" | custom-call | tf_op jit(solution)/shard_map/prolong/pallas_call | solution.py:281
  (2 shorter events, 0.0 us)
Async XLA Ops:
  0.6 9.4 %copy-start = (bf16[16,4,128,128]{3,2,1,0:T(8,128)(2,1)S(1)}, bf16[16,4,128,128]{3,2,1,0:T(8,128)(2,1)}, u32[]{:S(2)}) copy-start(bf16[16,4,128,128]{3,2,1,0:T(8,128)(2,1)} %w_ref.19) | copy-start | bytes 6291460
  0.8 0.8 %copy-start.4 = (s32[32]{0:T(128)S(1)}, s32[32]{0:T(128)}, u32[]{:S(2)}) copy-start(s32[32]{0:T(128)} %agg_ref.3) | copy-start | bytes 388
  1.5 7.1 %copy-start.2 = (s32[5]{0:T(128)}, s32[5]{0:T(128)S(1)}, u32[]{:S(2)}) copy-start(s32[5]{0:T(128)S(1)} %stack.31.mine_ref.info_ref) | copy-start | bytes 64
  1.5 11.7 %copy-start.1 = (f32[16,128]{1,0:T(8,128)S(1)}, f32[16,128]{1,0:T(8,128)}, u32[]{:S(2)}) copy-start(f32[16,128]{1,0:T(8,128)} %diag_ref.9) | copy-start | bytes 24580
  4.2 1.7 %collective-permute-start = (f32[16,16,128]{2,1,0:T(8,128)S(1)}, f32[16,16,128]{2,1,0:T(8,128)S(1)}, u32[]{:S(2)}, u32[]{:S(2)}) collective-permute-start(f32[16,16,128]{2,1,0:T(8,128)S(1)} %get-tuple-element.23), channel_id=1, source_target_pairs={{0,1},{1,0},{2,3},{3,2},{4,5},{5,4},{6,7},{7,6},{8,9},{9,8},{10,11... | collective-permute-start | bytes 393224 | tf_op jit(solution)/shard_map/ppermute | solution.py:240
  5.9 5.0 %collective-permute-start.2 = (bf16[16,16,128]{2,1,0:T(8,128)(2,1)S(1)}, bf16[16,16,128]{2,1,0:T(8,128)(2,1)S(1)}, u32[]{:S(2)}, u32[]{:S(2)}) collective-permute-start(bf16[16,16,128]{2,1,0:T(8,128)(2,1)S(1)} %fusion.q_ref), channel_id=1, source_target_pairs={{0,3},{3,0},{1,2},{2,1},{4,7},{7,4},{5,6},{6,5},{8,11},{11,8},{9,1... | collective-permute-start | bytes 196616 | tf_op jit(solution)/shard_map/ppermute | solution.py:252
  7.5 5.8 %collective-permute-start.1 = (bf16[16,16,128]{2,1,0:T(8,128)(2,1)S(1)}, bf16[16,16,128]{2,1,0:T(8,128)(2,1)}, u32[]{:S(2)}, u32[]{:S(2)}) collective-permute-start(bf16[16,16,128]{2,1,0:T(8,128)(2,1)S(1)} %fusion.q_ref), channel_id=1, source_target_pairs={{2,5},{5,2},{3,4},{4,3},{6,9},{9,6},{7,8},{8,7},{10,13},{13,10},{1... | collective-permute-start | bytes 196616 | tf_op jit(solution)/shard_map/ppermute | solution.py:251
  10.0 3.2 %copy-start.3 = (s32[5]{0:T(128)S(1)}, s32[5]{0:T(128)}, u32[]{:S(2)}) copy-start(s32[5]{0:T(128)} %copy-done.2) | copy-start | bytes 64
  14.4 3.9 %collective-permute-start.4 = (bf16[16,16,128]{2,1,0:T(8,128)(2,1)S(1)}, bf16[16,16,128]{2,1,0:T(8,128)(2,1)S(1)}, u32[]{:S(2)}, u32[]{:S(2)}) collective-permute-start(bf16[16,16,128]{2,1,0:T(8,128)(2,1)S(1)} %get-tuple-element.24.q_ref), channel_id=1, source_target_pairs={{0,3},{3,0},{1,2},{2,1},{4,7},{7,4},{5,6},{6,5},{8,11},{11,8},{9,1... | collective-permute-start | bytes 196616 | tf_op jit(solution)/shard_map/ppermute | solution.py:252
  15.2 5.7 %collective-permute-start.3 = (bf16[16,16,128]{2,1,0:T(8,128)(2,1)S(1)}, bf16[16,16,128]{2,1,0:T(8,128)(2,1)S(1)}, u32[]{:S(2)}, u32[]{:S(2)}) collective-permute-start(bf16[16,16,128]{2,1,0:T(8,128)(2,1)S(1)} %get-tuple-element.24.q_ref), channel_id=1, source_target_pairs={{2,5},{5,2},{3,4},{4,3},{6,9},{9,6},{7,8},{8,7},{10,13},{13,10},{1... | collective-permute-start | bytes 196616 | tf_op jit(solution)/shard_map/ppermute | solution.py:251
  21.8 4.1 %collective-permute-start.6 = (bf16[16,16,128]{2,1,0:T(8,128)(2,1)S(1)}, bf16[16,16,128]{2,1,0:T(8,128)(2,1)S(1)}, u32[]{:S(2)}, u32[]{:S(2)}) collective-permute-start(bf16[16,16,128]{2,1,0:T(8,128)(2,1)S(1)} %get-tuple-element.28.q_ref), channel_id=1, source_target_pairs={{0,3},{3,0},{1,2},{2,1},{4,7},{7,4},{5,6},{6,5},{8,11},{11,8},{9,1... | collective-permute-start | bytes 196616 | tf_op jit(solution)/shard_map/ppermute | solution.py:252
  22.2 5.7 %collective-permute-start.5 = (bf16[16,16,128]{2,1,0:T(8,128)(2,1)S(1)}, bf16[16,16,128]{2,1,0:T(8,128)(2,1)S(1)}, u32[]{:S(2)}, u32[]{:S(2)}) collective-permute-start(bf16[16,16,128]{2,1,0:T(8,128)(2,1)S(1)} %get-tuple-element.28.q_ref), channel_id=1, source_target_pairs={{2,5},{5,2},{3,4},{4,3},{6,9},{9,6},{7,8},{8,7},{10,13},{13,10},{1... | collective-permute-start | bytes 196616 | tf_op jit(solution)/shard_map/ppermute | solution.py:251
  28.8 3.9 %collective-permute-start.8 = (bf16[16,16,128]{2,1,0:T(8,128)(2,1)S(1)}, bf16[16,16,128]{2,1,0:T(8,128)(2,1)S(1)}, u32[]{:S(2)}, u32[]{:S(2)}) collective-permute-start(bf16[16,16,128]{2,1,0:T(8,128)(2,1)S(1)} %get-tuple-element.32.q_ref), channel_id=1, source_target_pairs={{0,3},{3,0},{1,2},{2,1},{4,7},{7,4},{5,6},{6,5},{8,11},{11,8},{9,1... | collective-permute-start | bytes 196616 | tf_op jit(solution)/shard_map/ppermute | solution.py:252
  29.6 5.7 %collective-permute-start.7 = (bf16[16,16,128]{2,1,0:T(8,128)(2,1)S(1)}, bf16[16,16,128]{2,1,0:T(8,128)(2,1)S(1)}, u32[]{:S(2)}, u32[]{:S(2)}) collective-permute-start(bf16[16,16,128]{2,1,0:T(8,128)(2,1)S(1)} %get-tuple-element.32.q_ref), channel_id=1, source_target_pairs={{2,5},{5,2},{3,4},{4,3},{6,9},{9,6},{7,8},{8,7},{10,13},{13,10},{1... | collective-permute-start | bytes 196616 | tf_op jit(solution)/shard_map/ppermute | solution.py:251
  36.2 8.4 %copy-start.5 = (s32[32]{0:T(128)S(1)}, s32[32]{0:T(128)}, u32[]{:S(2)}) copy-start(s32[32]{0:T(128)} %agg_ref.3) | copy-start | bytes 388
  36.2 3.9 %collective-permute-start.10 = (bf16[16,16,128]{2,1,0:T(8,128)(2,1)S(1)}, bf16[16,16,128]{2,1,0:T(8,128)(2,1)S(1)}, u32[]{:S(2)}, u32[]{:S(2)}) collective-permute-start(bf16[16,16,128]{2,1,0:T(8,128)(2,1)S(1)} %get-tuple-element.36.q_ref), channel_id=1, source_target_pairs={{0,3},{3,0},{1,2},{2,1},{4,7},{7,4},{5,6},{6,5},{8,11},{11,8},{9,1... | collective-permute-start | bytes 196616 | tf_op jit(solution)/shard_map/ppermute | solution.py:252
  36.6 5.7 %collective-permute-start.9 = (bf16[16,16,128]{2,1,0:T(8,128)(2,1)S(1)}, bf16[16,16,128]{2,1,0:T(8,128)(2,1)S(1)}, u32[]{:S(2)}, u32[]{:S(2)}) collective-permute-start(bf16[16,16,128]{2,1,0:T(8,128)(2,1)S(1)} %get-tuple-element.36.q_ref), channel_id=1, source_target_pairs={{2,5},{5,2},{3,4},{4,3},{6,9},{9,6},{7,8},{8,7},{10,13},{13,10},{1... | collective-permute-start | bytes 196616 | tf_op jit(solution)/shard_map/ppermute | solution.py:251
  43.2 1.4 %collective-permute-start.11 = (f32[16,16,128]{2,1,0:T(8,128)S(1)}, f32[16,16,128]{2,1,0:T(8,128)S(1)}, u32[]{:S(2)}, u32[]{:S(2)}) collective-permute-start(f32[16,16,128]{2,1,0:T(8,128)S(1)} %step.9.rest_0_), channel_id=1, source_target_pairs={{0,1},{1,0},{2,3},{3,2},{4,5},{5,4},{6,7},{7,6},{8,9},{9,8},{10,11... | collective-permute-start | bytes 393224 | tf_op jit(solution)/shard_map/ppermute | solution.py:279

commit v2 on v1

--- a/solution.py
+++ b/solution.py
@@ -70,14 +70,22 @@
     return pairs
 
 
+def table_layout(slots, blocks):
+    flags = 4 * slots + blocks
+    return dict(agg=4 * slots, mine=flags, odd_col=flags + 1, even_col=flags + 2,
+                odd_ok=flags + 3, even_ok=flags + 4, size=flags + 5)
+
+
 def restrict_kernel(
-    chunks, fine, agg_ref, mine_ref, res_hbm, pro_hbm, pro_ref, *rest
+    chunks, owners, fine, agg_hbm, nb_hbm, res_hbm, pro_hbm, pro_ref, tab_ref, *rest
 ):
     outs = rest[:fine]
-    res_ref, acc_ref, sems = rest[fine:]
+    agg_ref, nb_ref, res_ref, acc_ref, sems, small_sems = rest[fine:]
     blocks = pro_hbm.shape[0]
     size = blocks // chunks
+    slots = acc_ref.shape[1]
     share = acc_ref.shape[2]
+    where = table_layout(slots, blocks)
 
     def copies(c):
         part = pl.ds(c * size, size)
@@ -86,10 +94,31 @@
             pltpu.make_async_copy(res_hbm.at[part], res_ref.at[part], sems.at[1, c]),
         )
 
+    agg_copy = pltpu.make_async_copy(agg_hbm, agg_ref, small_sems.at[0])
+    nb_copy = pltpu.make_async_copy(nb_hbm, nb_ref, small_sems.at[1])
+    agg_copy.start()
     for c in range(chunks):
         for copy in copies(c):
             copy.start()
+    nb_copy.start()
+
+    owner = lax.axis_index("coarse")
+    k = lax.axis_index("fine")
+    is_odd = owner % 2 == 1
+    has_next = owner + 1 < owners
+    mine = jnp.where(is_odd, fine - 1 - k, k)
+    odd_col = jnp.where(is_odd, 3, 0)
+    even_col = jnp.where(is_odd, 0, 3)
+    tab_ref[where["mine"]] = mine
+    tab_ref[where["odd_col"]] = odd_col
+    tab_ref[where["even_col"]] = even_col
+    tab_ref[where["odd_ok"]] = jnp.where(is_odd, has_next, owner > 0).astype(jnp.int32)
+    tab_ref[where["even_ok"]] = jnp.where(is_odd, True, has_next).astype(jnp.int32)
+
     acc_ref[...] = jnp.zeros_like(acc_ref)
+    agg_copy.wait()
+    for i in range(blocks):
+        tab_ref[where["agg"] + i] = agg_ref[i]
     for c in range(chunks):
         for copy in copies(c):
             copy.wait()
@@ -103,34 +132,39 @@
             slot = agg_ref[i]
             for s in range(fine):
                 acc_ref[s, slot] += term[s * share : (s + 1) * share]
-    mine = mine_ref[0]
     for m in range(fine):
         outs[m][...] = acc_ref[mine ^ m]
-
-
-def own_kernel(nb_ref, w_ref, q_ref, out_ref):
+    nb_copy.wait()
+    odd_base = jnp.where(is_odd, 2 * slots, 0)
+    even_base = jnp.where(is_odd, 0, 2 * slots)
+    for b in range(slots):
+        tab_ref[b] = nb_ref[1, b] - slots
+        tab_ref[slots + b] = nb_ref[2, b] - slots
+        tab_ref[2 * slots + b] = nb_ref[odd_col, b] - odd_base
+        tab_ref[3 * slots + b] = nb_ref[even_col, b] - even_base
+
+
+def own_kernel(tab_ref, w_ref, q_ref, out_ref):
     slots = q_ref.shape[0]
     for b in range(slots):
-        left = jnp.concatenate(
-            [q_ref[nb_ref[b, 1] - slots], q_ref[nb_ref[b, 2] - slots]], axis=1
-        )
+        left = jnp.concatenate([q_ref[tab_ref[b]], q_ref[tab_ref[slots + b]]], axis=1)
         right = jnp.concatenate([w_ref[b, 1], w_ref[b, 2]], axis=0)
         out_ref[b] = jnp.dot(left, right, preferred_element_type=jnp.float32)
 
 
 def step_kernel(
-    keep, scale, last, info_ref, count_ref, nb_ref, w_ref, odd_ref, even_ref, own_ref, diag_ref,
+    keep, scale, last, where, count_ref, tab_ref, w_ref, odd_ref, even_ref, own_ref, diag_ref,
     rem_ref, upd_ref, sol_ref, *outs
 ):
     slots = own_ref.shape[0]
-    odd_col = info_ref[1]
-    even_col = info_ref[2]
-    odd_ok = info_ref[3]
-    even_ok = info_ref[4]
+    odd_col = tab_ref[where["odd_col"]]
+    even_col = tab_ref[where["even_col"]]
+    odd_ok = tab_ref[where["odd_ok"]]
+    even_ok = tab_ref[where["even_ok"]]
     count = count_ref[0]
     for b in range(slots):
-        odd = odd_ref[nb_ref[b, odd_col] % slots]
-        even = even_ref[nb_ref[b, even_col] % slots]
+        odd = odd_ref[tab_ref[2 * slots + b]]
+        even = even_ref[tab_ref[3 * slots + b]]
         odd = jnp.where(odd_ok > 0, odd, jnp.zeros_like(odd))
         even = jnp.where(even_ok > 0, even, jnp.zeros_like(even))
         left = jnp.concatenate([odd, even], axis=1)
@@ -150,11 +184,11 @@
             outs[3][b] = new.astype(outs[3].dtype)
 
 
-def prolong_kernel(chunks, fine, agg_ref, mine_ref, pro_ref, *rest):
+def prolong_kernel(chunks, fine, where, tab_ref, pro_ref, *rest):
     parts = rest[:fine]
-    cor_hbm, sol_ref, rounded_ref, cor_ref, sems = rest[fine:]
+    cor_hbm, sol_hbm, sol_ref, rounded_ref, cor_ref, sems, sol_sem = rest[fine:]
     share = parts[0].shape[1]
-    mine = mine_ref[0]
+    mine = tab_ref[where["mine"]]
     for s in range(fine):
         for m in range(fine):
             @pl.when((mine ^ m) == s)
@@ -162,6 +196,8 @@
                 piece = parts[m][...]
                 sol_ref[:, s * share : (s + 1) * share, :] = piece
                 rounded_ref[:, s * share : (s + 1) * share, :] = piece.astype(rounded_ref.dtype)
+    sol_copy = pltpu.make_async_copy(sol_ref, sol_hbm, sol_sem)
+    sol_copy.start()
     blocks = pro_ref.shape[0]
     size = blocks // chunks
 
@@ -172,9 +208,12 @@
     for c in range(chunks):
         for i in range(c * size, (c + 1) * size):
             cor_ref[i] = jnp.dot(
-                rounded_ref[agg_ref[i]], pro_ref[i], preferred_element_type=jnp.float32
+                rounded_ref[tab_ref[where["agg"] + i]],
+                pro_ref[i],
+                preferred_element_type=jnp.float32,
             )
         copy(c).start()
+    sol_copy.wait()
     for c in range(chunks):
         copy(c).wait()
 
@@ -198,42 +237,34 @@
     piece = (slots, share, width)
     middle, pairs = chebyshev_coefficients()
     chunks = 4
-
-    owner = lax.axis_index("coarse")
-    k = lax.axis_index("fine")
-    is_odd = owner % 2
-    mine = jnp.where(is_odd == 1, fine - 1 - k, k)
-    odd_ok = jnp.where(is_odd == 1, owner + 1 < owners, owner > 0)
-    even_ok = jnp.where(is_odd == 1, True, owner + 1 < owners)
-    info = jnp.stack(
-        [
-            mine,
-            jnp.where(is_odd == 1, 3, 0),
-            jnp.where(is_odd == 1, 0, 3),
-            odd_ok.astype(jnp.int32),
-            even_ok.astype(jnp.int32),
-        ]
-    ).astype(jnp.int32)
-    info = in_smem(info)
-    agg = in_smem(aggregate_map)
-    count = in_smem(block_counts)
-    nb = in_smem(neighbors)
-    weights = in_vmem(coarse_blocks)
-    diag = in_vmem(diag_values)
-
-    pro, *sums = pl.pallas_call(
-        functools.partial(restrict_kernel, chunks, fine),
-        out_shape=[VMEM(prolong_blocks.shape, bf16)] + [VMEM(piece, f32)] * fine,
-        in_specs=[smem_spec(), smem_spec()] + [pl.BlockSpec(memory_space=HBM)] * 2,
-        out_specs=[vmem_spec()] * (fine + 1),
+    where = table_layout(slots, blocks)
+
+    pro, tab, *sums = pl.pallas_call(
+        functools.partial(restrict_kernel, chunks, owners, fine),
+        out_shape=[VMEM(prolong_blocks.shape, bf16), SMEM((where["size"],), jnp.int32)]
+        + [VMEM(piece, f32)] * fine,
+        in_specs=[pl.BlockSpec(memory_space=HBM)] * 4,
+        out_specs=[vmem_spec(), smem_spec()] + [vmem_spec()] * fine,
         scratch_shapes=[
+            SMEM((blocks,), jnp.int32),
+            SMEM((neighbors.shape[1], slots), jnp.int32),
             VMEM(fine_residual.shape, bf16),
             VMEM((fine,) + piece, f32),
             pltpu.SemaphoreType.DMA((2, chunks)),
+            pltpu.SemaphoreType.DMA((2,)),
         ],
         compiler_params=params(8 * MIB),
         name="restrict",
-    )(agg, info, in_hbm(fine_residual), in_hbm(prolong_blocks))
+    )(
+        in_hbm(aggregate_map), in_hbm(neighbors.T),
+        in_hbm(fine_residual), in_hbm(prolong_blocks),
+    )
+    tab = in_smem(tab)
+    coarse_blocks, diag_values, sums[0] = lax.optimization_barrier(
+        (coarse_blocks, diag_values, sums[0])
+    )
+    weights = in_vmem(coarse_blocks)
+    diag = in_vmem(diag_values)
 
     coarse_rhs = sums[0]
     for m in range(1, fine):
@@ -257,17 +288,17 @@
             out_specs=vmem_spec(),
             compiler_params=params(4 * MIB),
             name="own",
-        )(nb, weights, in_vmem(q))
+        )(tab, weights, in_vmem(q))
         shapes = [VMEM(piece, f32)] if last else [VMEM(piece, f32)] * 3 + [VMEM(piece, bf16)]
         result = pl.pallas_call(
-            functools.partial(step_kernel, keep, scale, last),
+            functools.partial(step_kernel, keep, scale, last, where),
             out_shape=shapes,
-            in_specs=[smem_spec()] * 3 + [vmem_spec()] * 8,
+            in_specs=[smem_spec()] * 2 + [vmem_spec()] * 8,
             out_specs=[vmem_spec()] * len(shapes),
             compiler_params=params(4 * MIB),
             name="step",
         )(
-            info, count, nb, weights, in_vmem(odd), in_vmem(even), in_vmem(own), diag,
+            block_counts, tab, weights, in_vmem(odd), in_vmem(even), in_vmem(own), diag,
             in_vmem(rem), in_vmem(upd), in_vmem(sol),
         )
         if last:
@@ -279,21 +310,23 @@
         lax.ppermute(sol, "fine", [(a, a ^ m) for a in range(fine)]) for m in range(1, fine)
     ]
     correction, solution = pl.pallas_call(
-        functools.partial(prolong_kernel, chunks, fine),
+        functools.partial(prolong_kernel, chunks, fine, where),
         out_shape=[
             HBM(fine_residual.shape, f32),
-            jax.ShapeDtypeStruct((slots, rhs, width), f32),
+            HBM((slots, rhs, width), f32),
         ],
-        in_specs=[smem_spec(), smem_spec(), vmem_spec()] + [vmem_spec()] * fine,
-        out_specs=[pl.BlockSpec(memory_space=HBM), vmem_spec()],
+        in_specs=[smem_spec(), vmem_spec()] + [vmem_spec()] * fine,
+        out_specs=[pl.BlockSpec(memory_space=HBM)] * 2,
         scratch_shapes=[
+            VMEM((slots, rhs, width), f32),
             VMEM((slots, rhs, width), bf16),
             VMEM(fine_residual.shape, f32),
             pltpu.SemaphoreType.DMA((chunks,)),
+            pltpu.SemaphoreType.DMA,
         ],
         compiler_params=params(8 * MIB),
         name="prolong",
-    )(agg, info, in_vmem(pro), *[in_vmem(p) for p in parts])
+    )(tab, in_vmem(pro), *[in_vmem(p) for p in parts])
     return correction, solution
 
 

time: 47.2 us -> 40.9 us (0.87)
  Pallas kernels: 14.4 us -> 5.84 us
  waiting for transfers between devices: 19.4 us -> 21.8 us
    pallas_call x7, Pallas kernels: 9.91 us -> 4.63 us  [the longest x1 2.19 us: body(): pl.pallas_call(functools.partial(restrict_kernel, chunks, owners, fine),...]
    pallas_call x5, Pallas kernels: 4.54 us -> 1.21 us  [body(): pl.pallas_call(own_kernel, out_shape=VMEM(piece, f32), in_specs=[smem_spe...]
    ppermute x5, waiting for transfers between devices: 5.72 us -> 8.37 us  [body(): even = lax.ppermute(q, ('coarse', 'fine'), even_pairs)]
    unnamed x13 -> x4, local copies, waits for them, and re-layouts: 1.56 us -> 1.59 us
  transfers between devices with their start and end apart: 12 -> 12, of which waited for: 11 -> 11; matrix products, arithmetic and copies ran while one was open for 2% -> 0% of each run, Pallas kernels for 10% -> 3%
where the time goes in v2:
time: 40.9 us; the launch traced here: 40.7 us
  waiting for transfers between devices  21.8 us (53%)
  starting transfers between devices  10.1 us (25%)
  Pallas kernels  5.84 us (14%)
  local copies, waits for them, and re-layouts  1.59 us (4%)
  between operations  1.38 us (3%)
    ppermute x5, waiting for transfers between devices, body(): odd = lax.ppermute(q, ('coarse', 'fine'), odd_pairs)  11.2 us
    ppermute x5, waiting for transfers between devices, body(): even = lax.ppermute(q, ('coarse', 'fine'), even_pairs)  8.37 us
    ppermute x5, starting transfers between devices, body(): odd = lax.ppermute(q, ('coarse', 'fine'), odd_pairs)  5.19 us
    ppermute x5, starting transfers between devices, body(): even = lax.ppermute(q, ('coarse', 'fine'), even_pairs)  3.93 us
    pallas_call x1, Pallas kernels, body(): pl.pallas_call(functools.partial(restrict_kernel, chunks, owners, fine),...  2.19 us
    unnamed x4, local copies, waits for them, and re-layouts  1.59 us
    pallas_call x5, Pallas kernels, body(): pl.pallas_call(functools.partial(step_kernel, keep, scale, last, where),...  1.31 us
    pallas_call x5, Pallas kernels, body(): pl.pallas_call(own_kernel, out_shape=VMEM(piece, f32), in_specs=[smem_spe...  1.21 us
  transfers between devices with their start and end apart: 12, of which 11 were waited for; matrix products, arithmetic and copies ran while one was open for 0% of the time, Pallas kernels for 3%

profile of v2, /device:TPU:9, one launch (start us, length us, event | category | flops | bytes accessed | tf_op | source)
XLA Modules:
  0.0 40.7 jit_solution(18261111550157554703)
XLA Ops:
  0.6 0.0 copy-start.1
  0.6 2.2 %restrict.1 = (bf16[32,128,128]{2,1,0:T(8,128)(2,1)S(1)}, s32[101]{0:T(128)S(4)}, f32[16,16,128]{2,1,0:T(8,128)S(1)}, f32[16,16,128]{2,1,0:T(8,128)S(1)}) custom-call(s32[32]{0:T(128)} %agg_hbm.1, s32[4,16]{1,0:T(4,128)} %bitcast.1, bf16[32,32,128]{2,1,0:T(8,128)(2,1)} %res_hbm.1, bf16[32,128,128]{2,1,0:T(8,128)(2,1)} %pro_hbm.1), custom_call_target="tpu_custom_call" | custom-call | tf_op jit(solution)/shard_map/restrict/pallas_call | solution.py:242
  2.8 0.7 %collective-permute-start = (f32[16,16,128]{2,1,0:T(8,128)S(1)}, f32[16,16,128]{2,1,0:T(8,128)S(1)}, u32[]{:S(2)}, u32[]{:S(2)}) collective-permute-start(f32[16,16,128]{2,1,0:T(8,128)S(1)} %get-tuple-element.30), channel_id=1, source_target_pairs={{0,1},{1,0},{2,3},{3,2},{4,5},{5,4},{6,7},{7,6},{8,9},{9,8},{10,11... | collective-permute-start | bytes 393224 | tf_op jit(solution)/shard_map/ppermute | solution.py:271
  3.6 1.0 %collective-permute-done = f32[16,16,128]{2,1,0:T(8,128)S(1)} collective-permute-done((f32[16,16,128]{2,1,0:T(8,128)S(1)}, f32[16,16,128]{2,1,0:T(8,128)S(1)}, u32[]{:S(2)}, u32[]{:S(2)}) %collective-permute-start) | collective-permute-done | bytes 131104 | tf_op jit(solution)/shard_map/ppermute | solution.py:271
  4.6 1.5 %collective-permute-start.2 = (bf16[16,16,128]{2,1,0:T(8,128)(2,1)S(1)}, bf16[16,16,128]{2,1,0:T(8,128)(2,1)S(1)}, u32[]{:S(2)}, u32[]{:S(2)}) collective-permute-start(bf16[16,16,128]{2,1,0:T(8,128)(2,1)S(1)} %fusion.q_ref), channel_id=1, source_target_pairs={{0,3},{3,0},{1,2},{2,1},{4,7},{7,4},{5,6},{6,5},{8,11},{11,8},{9,1... | collective-permute-start | bytes 196616 | tf_op jit(solution)/shard_map/ppermute | solution.py:283
  6.1 1.1 %collective-permute-start.1 = (bf16[16,16,128]{2,1,0:T(8,128)(2,1)S(1)}, bf16[16,16,128]{2,1,0:T(8,128)(2,1)S(1)}, u32[]{:S(2)}, u32[]{:S(2)}) collective-permute-start(bf16[16,16,128]{2,1,0:T(8,128)(2,1)S(1)} %fusion.q_ref), channel_id=1, source_target_pairs={{2,5},{5,2},{3,4},{4,3},{6,9},{9,6},{7,8},{8,7},{10,13},{13,10},{1... | collective-permute-start | bytes 196616 | tf_op jit(solution)/shard_map/ppermute | solution.py:282
  7.9 0.0 copy-start
  7.9 1.6 %copy-done = bf16[16,4,128,128]{3,2,1,0:T(8,128)(2,1)S(1)} copy-done((bf16[16,4,128,128]{3,2,1,0:T(8,128)(2,1)S(1)}, bf16[16,4,128,128]{3,2,1,0:T(8,128)(2,1)}, u32[]{:S(2)}) %copy-start) | copy-done | bytes 2097176
  9.5 0.2 own.5.own_ref
  9.8 0.0 collective-permute-done.2.even_ref
  9.8 2.0 %collective-permute-done.1.odd_ref = bf16[16,16,128]{2,1,0:T(8,128)(2,1)S(1)} collective-permute-done((bf16[16,16,128]{2,1,0:T(8,128)(2,1)S(1)}, bf16[16,16,128]{2,1,0:T(8,128)(2,1)S(1)}, u32[]{:S(2)}, u32[]{:S(2)}) %collective-permute-start.1) | collective-permute-done | bytes 65568 | tf_op jit(solution)/shard_map/ppermute | solution.py:282
  11.8 0.0 copy-done.1
  11.8 0.3 step.5
  12.1 0.8 %collective-permute-start.4 = (bf16[16,16,128]{2,1,0:T(8,128)(2,1)S(1)}, bf16[16,16,128]{2,1,0:T(8,128)(2,1)S(1)}, u32[]{:S(2)}, u32[]{:S(2)}) collective-permute-start(bf16[16,16,128]{2,1,0:T(8,128)(2,1)S(1)} %get-tuple-element.32.q_ref), channel_id=1, source_target_pairs={{0,3},{3,0},{1,2},{2,1},{4,7},{7,4},{5,6},{6,5},{8,11},{11,8},{9,1... | collective-permute-start | bytes 196616 | tf_op jit(solution)/shard_map/ppermute | solution.py:283
  12.9 0.9 %collective-permute-start.3 = (bf16[16,16,128]{2,1,0:T(8,128)(2,1)S(1)}, bf16[16,16,128]{2,1,0:T(8,128)(2,1)S(1)}, u32[]{:S(2)}, u32[]{:S(2)}) collective-permute-start(bf16[16,16,128]{2,1,0:T(8,128)(2,1)S(1)} %get-tuple-element.32.q_ref), channel_id=1, source_target_pairs={{2,5},{5,2},{3,4},{4,3},{6,9},{9,6},{7,8},{8,7},{10,13},{13,10},{1... | collective-permute-start | bytes 196616 | tf_op jit(solution)/shard_map/ppermute | solution.py:282
  13.8 0.2 own.6.own_ref
  14.1 1.9 %collective-permute-done.4.even_ref = bf16[16,16,128]{2,1,0:T(8,128)(2,1)S(1)} collective-permute-done((bf16[16,16,128]{2,1,0:T(8,128)(2,1)S(1)}, bf16[16,16,128]{2,1,0:T(8,128)(2,1)S(1)}, u32[]{:S(2)}, u32[]{:S(2)}) %collective-permute-start.4) | collective-permute-done | bytes 65568 | tf_op jit(solution)/shard_map/ppermute | solution.py:283
  16.0 2.6 %collective-permute-done.3.odd_ref = bf16[16,16,128]{2,1,0:T(8,128)(2,1)S(1)} collective-permute-done((bf16[16,16,128]{2,1,0:T(8,128)(2,1)S(1)}, bf16[16,16,128]{2,1,0:T(8,128)(2,1)S(1)}, u32[]{:S(2)}, u32[]{:S(2)}) %collective-permute-start.3) | collective-permute-done | bytes 65568 | tf_op jit(solution)/shard_map/ppermute | solution.py:282
  18.6 0.3 step.6
  18.8 0.4 collective-permute-start.6
  19.2 1.1 %collective-permute-start.5 = (bf16[16,16,128]{2,1,0:T(8,128)(2,1)S(1)}, bf16[16,16,128]{2,1,0:T(8,128)(2,1)S(1)}, u32[]{:S(2)}, u32[]{:S(2)}) collective-permute-start(bf16[16,16,128]{2,1,0:T(8,128)(2,1)S(1)} %get-tuple-element.36.q_ref), channel_id=1, source_target_pairs={{2,5},{5,2},{3,4},{4,3},{6,9},{9,6},{7,8},{8,7},{10,13},{13,10},{1... | collective-permute-start | bytes 196616 | tf_op jit(solution)/shard_map/ppermute | solution.py:282
  20.3 0.2 own.7.own_ref
  20.6 2.3 %collective-permute-done.6.even_ref = bf16[16,16,128]{2,1,0:T(8,128)(2,1)S(1)} collective-permute-done((bf16[16,16,128]{2,1,0:T(8,128)(2,1)S(1)}, bf16[16,16,128]{2,1,0:T(8,128)(2,1)S(1)}, u32[]{:S(2)}, u32[]{:S(2)}) %collective-permute-start.6) | collective-permute-done | bytes 65568 | tf_op jit(solution)/shard_map/ppermute | solution.py:283
  22.9 1.9 %collective-permute-done.5.odd_ref = bf16[16,16,128]{2,1,0:T(8,128)(2,1)S(1)} collective-permute-done((bf16[16,16,128]{2,1,0:T(8,128)(2,1)S(1)}, bf16[16,16,128]{2,1,0:T(8,128)(2,1)S(1)}, u32[]{:S(2)}, u32[]{:S(2)}) %collective-permute-start.5) | collective-permute-done | bytes 65568 | tf_op jit(solution)/shard_map/ppermute | solution.py:282
  24.8 0.3 step.7
  25.1 0.8 %collective-permute-start.8 = (bf16[16,16,128]{2,1,0:T(8,128)(2,1)S(1)}, bf16[16,16,128]{2,1,0:T(8,128)(2,1)S(1)}, u32[]{:S(2)}, u32[]{:S(2)}) collective-permute-start(bf16[16,16,128]{2,1,0:T(8,128)(2,1)S(1)} %get-tuple-element.40.q_ref), channel_id=1, source_target_pairs={{0,3},{3,0},{1,2},{2,1},{4,7},{7,4},{5,6},{6,5},{8,11},{11,8},{9,1... | collective-permute-start | bytes 196616 | tf_op jit(solution)/shard_map/ppermute | solution.py:283
  25.9 0.9 %collective-permute-start.7 = (bf16[16,16,128]{2,1,0:T(8,128)(2,1)S(1)}, bf16[16,16,128]{2,1,0:T(8,128)(2,1)S(1)}, u32[]{:S(2)}, u32[]{:S(2)}) collective-permute-start(bf16[16,16,128]{2,1,0:T(8,128)(2,1)S(1)} %get-tuple-element.40.q_ref), channel_id=1, source_target_pairs={{2,5},{5,2},{3,4},{4,3},{6,9},{9,6},{7,8},{8,7},{10,13},{13,10},{1... | collective-permute-start | bytes 196616 | tf_op jit(solution)/shard_map/ppermute | solution.py:282
  26.9 0.2 own.8.own_ref
  27.1 1.9 %collective-permute-done.8.even_ref = bf16[16,16,128]{2,1,0:T(8,128)(2,1)S(1)} collective-permute-done((bf16[16,16,128]{2,1,0:T(8,128)(2,1)S(1)}, bf16[16,16,128]{2,1,0:T(8,128)(2,1)S(1)}, u32[]{:S(2)}, u32[]{:S(2)}) %collective-permute-start.8) | collective-permute-done | bytes 65568 | tf_op jit(solution)/shard_map/ppermute | solution.py:283
  29.0 2.6 %collective-permute-done.7.odd_ref = bf16[16,16,128]{2,1,0:T(8,128)(2,1)S(1)} collective-permute-done((bf16[16,16,128]{2,1,0:T(8,128)(2,1)S(1)}, bf16[16,16,128]{2,1,0:T(8,128)(2,1)S(1)}, u32[]{:S(2)}, u32[]{:S(2)}) %collective-permute-start.7) | collective-permute-done | bytes 65568 | tf_op jit(solution)/shard_map/ppermute | solution.py:282
  31.6 0.3 step.8
  31.9 0.4 collective-permute-start.10
  32.2 1.1 %collective-permute-start.9 = (bf16[16,16,128]{2,1,0:T(8,128)(2,1)S(1)}, bf16[16,16,128]{2,1,0:T(8,128)(2,1)S(1)}, u32[]{:S(2)}, u32[]{:S(2)}) collective-permute-start(bf16[16,16,128]{2,1,0:T(8,128)(2,1)S(1)} %get-tuple-element.44.q_ref), channel_id=1, source_target_pairs={{2,5},{5,2},{3,4},{4,3},{6,9},{9,6},{7,8},{8,7},{10,13},{13,10},{1... | collective-permute-start | bytes 196616 | tf_op jit(solution)/shard_map/ppermute | solution.py:282
  33.3 0.2 own.9.own_ref
  33.6 2.2 %collective-permute-done.10.even_ref = bf16[16,16,128]{2,1,0:T(8,128)(2,1)S(1)} collective-permute-done((bf16[16,16,128]{2,1,0:T(8,128)(2,1)S(1)}, bf16[16,16,128]{2,1,0:T(8,128)(2,1)S(1)}, u32[]{:S(2)}, u32[]{:S(2)}) %collective-permute-start.10) | collective-permute-done | bytes 65568 | tf_op jit(solution)/shard_map/ppermute | solution.py:283
  35.8 2.1 %collective-permute-done.9.odd_ref = bf16[16,16,128]{2,1,0:T(8,128)(2,1)S(1)} collective-permute-done((bf16[16,16,128]{2,1,0:T(8,128)(2,1)S(1)}, bf16[16,16,128]{2,1,0:T(8,128)(2,1)S(1)}, u32[]{:S(2)}, u32[]{:S(2)}) %collective-permute-start.9) | collective-permute-done | bytes 65568 | tf_op jit(solution)/shard_map/ppermute | solution.py:282
  37.9 0.3 step.9.rest_0_
  38.1 0.2 collective-permute-start.11
  38.3 1.2 %collective-permute-done.11.rest_1_ = f32[16,16,128]{2,1,0:T(8,128)S(1)} collective-permute-done((f32[16,16,128]{2,1,0:T(8,128)S(1)}, f32[16,16,128]{2,1,0:T(8,128)S(1)}, u32[]{:S(2)}, u32[]{:S(2)}) %collective-permute-start.11) | collective-permute-done | bytes 131104 | tf_op jit(solution)/shard_map/ppermute | solution.py:310
  39.6 1.1 %prolong.1 = (f32[32,32,128]{2,1,0:T(8,128)}, f32[16,32,128]{2,1,0:T(8,128)}) custom-call(s32[101]{0:T(128)S(4)} %get-tuple-element.25.tab_ref, bf16[32,128,128]{2,1,0:T(8,128)(2,1)S(1)} %get-tuple-element.26.pro_ref, f32[16,16,128]{2,1,0:T(8,128)S(1)} %step.9.rest_0_, f32[16,16,128]{2,1,0:T(8,128)S(1)} %collective-permute-done.11.rest_1_), custom_call_target="tpu_custom_call" | custom-call | tf_op jit(solution)/shard_map/prolong/pallas_call | solution.py:312
  (2 shorter events, 0.0 us)
Async XLA Ops:
  0.6 11.2 %copy-start.1 = (f32[16,128]{1,0:T(8,128)S(1)}, f32[16,128]{1,0:T(8,128)}, u32[]{:S(2)}) copy-start(f32[16,128]{1,0:T(8,128)} %diag_ref.4) | copy-start | bytes 24580
  2.8 1.7 %collective-permute-start = (f32[16,16,128]{2,1,0:T(8,128)S(1)}, f32[16,16,128]{2,1,0:T(8,128)S(1)}, u32[]{:S(2)}, u32[]{:S(2)}) collective-permute-start(f32[16,16,128]{2,1,0:T(8,128)S(1)} %get-tuple-element.30), channel_id=1, source_target_pairs={{0,1},{1,0},{2,3},{3,2},{4,5},{5,4},{6,7},{7,6},{8,9},{9,8},{10,11... | collective-permute-start | bytes 393224 | tf_op jit(solution)/shard_map/ppermute | solution.py:271
  4.6 5.1 %collective-permute-start.2 = (bf16[16,16,128]{2,1,0:T(8,128)(2,1)S(1)}, bf16[16,16,128]{2,1,0:T(8,128)(2,1)S(1)}, u32[]{:S(2)}, u32[]{:S(2)}) collective-permute-start(bf16[16,16,128]{2,1,0:T(8,128)(2,1)S(1)} %fusion.q_ref), channel_id=1, source_target_pairs={{0,3},{3,0},{1,2},{2,1},{4,7},{7,4},{5,6},{6,5},{8,11},{11,8},{9,1... | collective-permute-start | bytes 196616 | tf_op jit(solution)/shard_map/ppermute | solution.py:283
  6.1 5.6 %collective-permute-start.1 = (bf16[16,16,128]{2,1,0:T(8,128)(2,1)S(1)}, bf16[16,16,128]{2,1,0:T(8,128)(2,1)S(1)}, u32[]{:S(2)}, u32[]{:S(2)}) collective-permute-start(bf16[16,16,128]{2,1,0:T(8,128)(2,1)S(1)} %fusion.q_ref), channel_id=1, source_target_pairs={{2,5},{5,2},{3,4},{4,3},{6,9},{9,6},{7,8},{8,7},{10,13},{13,10},{1... | collective-permute-start | bytes 196616 | tf_op jit(solution)/shard_map/ppermute | solution.py:282
  7.9 1.6 %copy-start = (bf16[16,4,128,128]{3,2,1,0:T(8,128)(2,1)S(1)}, bf16[16,4,128,128]{3,2,1,0:T(8,128)(2,1)}, u32[]{:S(2)}) copy-start(bf16[16,4,128,128]{3,2,1,0:T(8,128)(2,1)} %w_ref.9) | copy-start | bytes 6291460
  12.1 3.9 %collective-permute-start.4 = (bf16[16,16,128]{2,1,0:T(8,128)(2,1)S(1)}, bf16[16,16,128]{2,1,0:T(8,128)(2,1)S(1)}, u32[]{:S(2)}, u32[]{:S(2)}) collective-permute-start(bf16[16,16,128]{2,1,0:T(8,128)(2,1)S(1)} %get-tuple-element.32.q_ref), channel_id=1, source_target_pairs={{0,3},{3,0},{1,2},{2,1},{4,7},{7,4},{5,6},{6,5},{8,11},{11,8},{9,1... | collective-permute-start | bytes 196616 | tf_op jit(solution)/shard_map/ppermute | solution.py:283
  12.9 5.7 %collective-permute-start.3 = (bf16[16,16,128]{2,1,0:T(8,128)(2,1)S(1)}, bf16[16,16,128]{2,1,0:T(8,128)(2,1)S(1)}, u32[]{:S(2)}, u32[]{:S(2)}) collective-permute-start(bf16[16,16,128]{2,1,0:T(8,128)(2,1)S(1)} %get-tuple-element.32.q_ref), channel_id=1, source_target_pairs={{2,5},{5,2},{3,4},{4,3},{6,9},{9,6},{7,8},{8,7},{10,13},{13,10},{1... | collective-permute-start | bytes 196616 | tf_op jit(solution)/shard_map/ppermute | solution.py:282
  18.8 4.1 %collective-permute-start.6 = (bf16[16,16,128]{2,1,0:T(8,128)(2,1)S(1)}, bf16[16,16,128]{2,1,0:T(8,128)(2,1)S(1)}, u32[]{:S(2)}, u32[]{:S(2)}) collective-permute-start(bf16[16,16,128]{2,1,0:T(8,128)(2,1)S(1)} %get-tuple-element.36.q_ref), channel_id=1, source_target_pairs={{0,3},{3,0},{1,2},{2,1},{4,7},{7,4},{5,6},{6,5},{8,11},{11,8},{9,1... | collective-permute-start | bytes 196616 | tf_op jit(solution)/shard_map/ppermute | solution.py:283
  19.2 5.6 %collective-permute-start.5 = (bf16[16,16,128]{2,1,0:T(8,128)(2,1)S(1)}, bf16[16,16,128]{2,1,0:T(8,128)(2,1)S(1)}, u32[]{:S(2)}, u32[]{:S(2)}) collective-permute-start(bf16[16,16,128]{2,1,0:T(8,128)(2,1)S(1)} %get-tuple-element.36.q_ref), channel_id=1, source_target_pairs={{2,5},{5,2},{3,4},{4,3},{6,9},{9,6},{7,8},{8,7},{10,13},{13,10},{1... | collective-permute-start | bytes 196616 | tf_op jit(solution)/shard_map/ppermute | solution.py:282
  25.1 3.9 %collective-permute-start.8 = (bf16[16,16,128]{2,1,0:T(8,128)(2,1)S(1)}, bf16[16,16,128]{2,1,0:T(8,128)(2,1)S(1)}, u32[]{:S(2)}, u32[]{:S(2)}) collective-permute-start(bf16[16,16,128]{2,1,0:T(8,128)(2,1)S(1)} %get-tuple-element.40.q_ref), channel_id=1, source_target_pairs={{0,3},{3,0},{1,2},{2,1},{4,7},{7,4},{5,6},{6,5},{8,11},{11,8},{9,1... | collective-permute-start | bytes 196616 | tf_op jit(solution)/shard_map/ppermute | solution.py:283
  25.9 5.7 %collective-permute-start.7 = (bf16[16,16,128]{2,1,0:T(8,128)(2,1)S(1)}, bf16[16,16,128]{2,1,0:T(8,128)(2,1)S(1)}, u32[]{:S(2)}, u32[]{:S(2)}) collective-permute-start(bf16[16,16,128]{2,1,0:T(8,128)(2,1)S(1)} %get-tuple-element.40.q_ref), channel_id=1, source_target_pairs={{2,5},{5,2},{3,4},{4,3},{6,9},{9,6},{7,8},{8,7},{10,13},{13,10},{1... | collective-permute-start | bytes 196616 | tf_op jit(solution)/shard_map/ppermute | solution.py:282
  31.9 3.9 %collective-permute-start.10 = (bf16[16,16,128]{2,1,0:T(8,128)(2,1)S(1)}, bf16[16,16,128]{2,1,0:T(8,128)(2,1)S(1)}, u32[]{:S(2)}, u32[]{:S(2)}) collective-permute-start(bf16[16,16,128]{2,1,0:T(8,128)(2,1)S(1)} %get-tuple-element.44.q_ref), channel_id=1, source_target_pairs={{0,3},{3,0},{1,2},{2,1},{4,7},{7,4},{5,6},{6,5},{8,11},{11,8},{9,1... | collective-permute-start | bytes 196616 | tf_op jit(solution)/shard_map/ppermute | solution.py:283
  32.2 5.6 %collective-permute-start.9 = (bf16[16,16,128]{2,1,0:T(8,128)(2,1)S(1)}, bf16[16,16,128]{2,1,0:T(8,128)(2,1)S(1)}, u32[]{:S(2)}, u32[]{:S(2)}) collective-permute-start(bf16[16,16,128]{2,1,0:T(8,128)(2,1)S(1)} %get-tuple-element.44.q_ref), channel_id=1, source_target_pairs={{2,5},{5,2},{3,4},{4,3},{6,9},{9,6},{7,8},{8,7},{10,13},{13,10},{1... | collective-permute-start | bytes 196616 | tf_op jit(solution)/shard_map/ppermute | solution.py:282
  38.1 1.4 %collective-permute-start.11 = (f32[16,16,128]{2,1,0:T(8,128)S(1)}, f32[16,16,128]{2,1,0:T(8,128)S(1)}, u32[]{:S(2)}, u32[]{:S(2)}) collective-permute-start(f32[16,16,128]{2,1,0:T(8,128)S(1)} %step.9.rest_0_), channel_id=1, source_target_pairs={{0,1},{1,0},{2,3},{3,2},{4,5},{5,4},{6,7},{7,6},{8,9},{9,8},{10,11... | collective-permute-start | bytes 393224 | tf_op jit(solution)/shard_map/ppermute | solution.py:310

commit v3 on v2

--- a/solution.py
+++ b/solution.py
@@ -70,6 +70,17 @@
     return pairs
 
 
+def on_diagonal(rows):
+    blank = jnp.zeros_like(rows[0])
+    return jnp.concatenate(
+        [
+            jnp.concatenate([row if i == j else blank for j in range(len(rows))], axis=1)
+            for i, row in enumerate(rows)
+        ],
+        axis=0,
+    )
+
+
 def table_layout(slots, blocks):
     flags = 4 * slots + blocks
     return dict(agg=4 * slots, mine=flags, odd_col=flags + 1, even_col=flags + 2,
@@ -87,19 +98,17 @@
     share = acc_ref.shape[2]
     where = table_layout(slots, blocks)
 
-    def copies(c):
+    def pro_copy(c):
         part = pl.ds(c * size, size)
-        return (
-            pltpu.make_async_copy(pro_hbm.at[part], pro_ref.at[part], sems.at[0, c]),
-            pltpu.make_async_copy(res_hbm.at[part], res_ref.at[part], sems.at[1, c]),
-        )
-
+        return pltpu.make_async_copy(pro_hbm.at[part], pro_ref.at[part], sems.at[c])
+
+    res_copy = pltpu.make_async_copy(res_hbm, res_ref, small_sems.at[2])
     agg_copy = pltpu.make_async_copy(agg_hbm, agg_ref, small_sems.at[0])
     nb_copy = pltpu.make_async_copy(nb_hbm, nb_ref, small_sems.at[1])
+    res_copy.start()
+    for c in range(chunks):
+        pro_copy(c).start()
     agg_copy.start()
-    for c in range(chunks):
-        for copy in copies(c):
-            copy.start()
     nb_copy.start()
 
     owner = lax.axis_index("coarse")
@@ -109,6 +118,8 @@
     mine = jnp.where(is_odd, fine - 1 - k, k)
     odd_col = jnp.where(is_odd, 3, 0)
     even_col = jnp.where(is_odd, 0, 3)
+    odd_base = jnp.where(is_odd, 2 * slots, 0)
+    even_base = jnp.where(is_odd, 0, 2 * slots)
     tab_ref[where["mine"]] = mine
     tab_ref[where["odd_col"]] = odd_col
     tab_ref[where["even_col"]] = even_col
@@ -116,72 +127,104 @@
     tab_ref[where["even_ok"]] = jnp.where(is_odd, True, has_next).astype(jnp.int32)
 
     acc_ref[...] = jnp.zeros_like(acc_ref)
-    agg_copy.wait()
-    for i in range(blocks):
-        tab_ref[where["agg"] + i] = agg_ref[i]
-    for c in range(chunks):
-        for copy in copies(c):
-            copy.wait()
-        for i in range(c * size, (c + 1) * size):
-            term = lax.dot_general(
-                res_ref[i],
-                pro_ref[i],
-                (((1,), (1,)), ((), ())),
-                preferred_element_type=jnp.float32,
-            )
-            slot = agg_ref[i]
-            for s in range(fine):
-                acc_ref[s, slot] += term[s * share : (s + 1) * share]
-    for m in range(fine):
-        outs[m][...] = acc_ref[mine ^ m]
     nb_copy.wait()
-    odd_base = jnp.where(is_odd, 2 * slots, 0)
-    even_base = jnp.where(is_odd, 0, 2 * slots)
     for b in range(slots):
         tab_ref[b] = nb_ref[1, b] - slots
         tab_ref[slots + b] = nb_ref[2, b] - slots
         tab_ref[2 * slots + b] = nb_ref[odd_col, b] - odd_base
         tab_ref[3 * slots + b] = nb_ref[even_col, b] - even_base
-
-
-def own_kernel(tab_ref, w_ref, q_ref, out_ref):
+    agg_copy.wait()
+    for i in range(blocks):
+        tab_ref[where["agg"] + i] = agg_ref[i]
+    res_copy.wait()
+    rhs = res_hbm.shape[1]
+    group = 2 if size % 2 == 0 else 1
+    for c in range(chunks):
+        pro_copy(c).wait()
+        for first in range(c * size, (c + 1) * size, group):
+            members = range(first, first + group)
+            terms = lax.dot_general(
+                on_diagonal([res_ref[i] for i in members]),
+                jnp.concatenate([pro_ref[i] for i in members], axis=1),
+                (((1,), (1,)), ((), ())),
+                preferred_element_type=jnp.float32,
+            )
+            for j, i in enumerate(members):
+                slot = agg_ref[i]
+                for s in range(fine):
+                    top = j * rhs + s * share
+                    acc_ref[s, slot] += terms[top : top + share]
+    for m in range(fine):
+        outs[m][...] = acc_ref[mine ^ m]
+
+
+def mid_kernel(first, before, keep, scale, middle, where, count_ref, tab_ref, w_ref, q_ref,
+               even_ref, diag_ref, *refs):
+    state, outs = refs[: 1 if first else 4], refs[1 if first else 4 :]
     slots = q_ref.shape[0]
-    for b in range(slots):
-        left = jnp.concatenate([q_ref[tab_ref[b]], q_ref[tab_ref[slots + b]]], axis=1)
-        right = jnp.concatenate([w_ref[b, 1], w_ref[b, 2]], axis=0)
-        out_ref[b] = jnp.dot(left, right, preferred_element_type=jnp.float32)
-
-
-def step_kernel(
-    keep, scale, last, where, count_ref, tab_ref, w_ref, odd_ref, even_ref, own_ref, diag_ref,
-    rem_ref, upd_ref, sol_ref, *outs
-):
-    slots = own_ref.shape[0]
-    odd_col = tab_ref[where["odd_col"]]
     even_col = tab_ref[where["even_col"]]
-    odd_ok = tab_ref[where["odd_ok"]]
     even_ok = tab_ref[where["even_ok"]]
     count = count_ref[0]
     for b in range(slots):
-        odd = odd_ref[tab_ref[2 * slots + b]]
         even = even_ref[tab_ref[3 * slots + b]]
-        odd = jnp.where(odd_ok > 0, odd, jnp.zeros_like(odd))
         even = jnp.where(even_ok > 0, even, jnp.zeros_like(even))
-        left = jnp.concatenate([odd, even], axis=1)
-        right = jnp.concatenate([w_ref[b, odd_col], w_ref[b, even_col]], axis=0)
-        coupled = own_ref[b] + jnp.dot(left, right, preferred_element_type=jnp.float32)
-        upd = upd_ref[b]
+        left = jnp.concatenate(
+            [q_ref[tab_ref[b]], q_ref[tab_ref[slots + b]], even], axis=1
+        )
+        right = jnp.concatenate([w_ref[b, 1], w_ref[b, 2], w_ref[b, even_col]], axis=0)
+        coupled = jnp.dot(left, right, preferred_element_type=jnp.float32)
+        if first:
+            rem = state[0][b]
+            upd = rem / middle
+            sol = upd
+        else:
+            late = state[3][b]
+            rem = state[0][b] - late
+            upd = state[1][b] - before * late
+            sol = state[2][b] - before * late
         applied = diag_ref[b : b + 1, :] * upd + coupled
-        rem = rem_ref[b] - jnp.where(b < count, applied, jnp.zeros_like(applied))
-        new = keep * upd + scale * rem
-        sol = sol_ref[b] + new
-        if last:
-            outs[0][b] = sol
-        else:
-            outs[0][b] = rem
-            outs[1][b] = new
-            outs[2][b] = sol
-            outs[3][b] = new.astype(outs[3].dtype)
+        rem = rem - jnp.where(b < count, applied, jnp.zeros_like(applied))
+        base = keep * upd + scale * rem
+        outs[0][b] = sol + base
+        if len(outs) > 1:
+            outs[1][b] = rem
+            outs[2][b] = base
+
+
+def step_kernel(scale, last, where, count_ref, tab_ref, w_ref, odd_ref, base_ref, *outs):
+    slots, share, _ = odd_ref.shape
+    odd_col = tab_ref[where["odd_col"]]
+    live = jnp.where(tab_ref[where["odd_ok"]] > 0, count_ref[0], 0)
+    group = 2 if slots % 2 == 0 else 1
+    for first in range(0, slots, group):
+        members = range(first, first + group)
+        left = on_diagonal([odd_ref[tab_ref[2 * slots + b]] for b in members])
+        right = jnp.concatenate([w_ref[b, odd_col] for b in members], axis=0)
+        both = jnp.dot(left, right, preferred_element_type=jnp.float32)
+        for i, b in enumerate(members):
+            late = both[i * share : (i + 1) * share]
+            late = jnp.where(b < live, late, jnp.zeros_like(late))
+            new = base_ref[b] - scale * late
+            if last:
+                outs[0][b] = new
+            else:
+                outs[0][b] = late
+                outs[1][b] = new.astype(outs[1].dtype)
+
+
+def load_kernel(chunks, after_ref, w_hbm, diag_hbm, w_ref, diag_ref, sems, diag_sem):
+    size = w_hbm.shape[0] // chunks
+    copies = [
+        pltpu.make_async_copy(
+            w_hbm.at[pl.ds(c * size, size)], w_ref.at[pl.ds(c * size, size)], sems.at[c]
+        )
+        for c in range(chunks)
+    ]
+    copies.append(pltpu.make_async_copy(diag_hbm, diag_ref, diag_sem))
+    for copy in copies:
+        copy.start()
+    for copy in copies:
+        copy.wait()
 
 
 def prolong_kernel(chunks, fine, where, tab_ref, pro_ref, *rest):
@@ -200,18 +243,23 @@
     sol_copy.start()
     blocks = pro_ref.shape[0]
     size = blocks // chunks
+    rhs = rounded_ref.shape[1]
+    group = 2 if size % 2 == 0 else 1
 
     def copy(c):
         part = pl.ds(c * size, size)
         return pltpu.make_async_copy(cor_ref.at[part], cor_hbm.at[part], sems.at[c])
 
     for c in range(chunks):
-        for i in range(c * size, (c + 1) * size):
-            cor_ref[i] = jnp.dot(
-                rounded_ref[tab_ref[where["agg"] + i]],
-                pro_ref[i],
+        for first in range(c * size, (c + 1) * size, group):
+            members = range(first, first + group)
+            both = jnp.dot(
+                on_diagonal([rounded_ref[tab_ref[where["agg"] + i]] for i in members]),
+                jnp.concatenate([pro_ref[i] for i in members], axis=0),
                 preferred_element_type=jnp.float32,
             )
+            for j, i in enumerate(members):
+                cor_ref[i] = both[j * rhs : (j + 1) * rhs]
         copy(c).start()
     sol_copy.wait()
     for c in range(chunks):
@@ -236,7 +284,7 @@
     bf16 = jnp.bfloat16
     piece = (slots, share, width)
     middle, pairs = chebyshev_coefficients()
-    chunks = 4
+    chunks = 2
     where = table_layout(slots, blocks)
 
     pro, tab, *sums = pl.pallas_call(
@@ -250,8 +298,8 @@
             SMEM((neighbors.shape[1], slots), jnp.int32),
             VMEM(fine_residual.shape, bf16),
             VMEM((fine,) + piece, f32),
-            pltpu.SemaphoreType.DMA((2, chunks)),
-            pltpu.SemaphoreType.DMA((2,)),
+            pltpu.SemaphoreType.DMA((chunks,)),
+            pltpu.SemaphoreType.DMA((3,)),
         ],
         compiler_params=params(8 * MIB),
         name="restrict",
@@ -260,51 +308,59 @@
         in_hbm(fine_residual), in_hbm(prolong_blocks),
     )
     tab = in_smem(tab)
-    coarse_blocks, diag_values, sums[0] = lax.optimization_barrier(
-        (coarse_blocks, diag_values, sums[0])
-    )
-    weights = in_vmem(coarse_blocks)
-    diag = in_vmem(diag_values)
-
     coarse_rhs = sums[0]
     for m in range(1, fine):
         coarse_rhs = coarse_rhs + lax.ppermute(
             sums[m], "fine", [(a, a ^ m) for a in range(fine)]
         )
-    rem = coarse_rhs
-    upd = coarse_rhs / middle
-    sol = upd
-    q = upd.astype(bf16)
+    state = [coarse_rhs]
+    q = (coarse_rhs / middle).astype(bf16)
+    before = 0.0
     odd_pairs = swap_pairs(1, owners, fine)
     even_pairs = swap_pairs(0, owners, fine)
     for t, (keep, scale) in enumerate(pairs):
         last = t == len(pairs) - 1
         odd = lax.ppermute(q, ("coarse", "fine"), odd_pairs)
         even = lax.ppermute(q, ("coarse", "fine"), even_pairs)
-        own = pl.pallas_call(
-            own_kernel,
-            out_shape=VMEM(piece, f32),
-            in_specs=[smem_spec(), vmem_spec(), vmem_spec()],
-            out_specs=vmem_spec(),
+        if t == 0:
+            weights, diag = pl.pallas_call(
+                functools.partial(load_kernel, chunks),
+                out_shape=[VMEM(coarse_blocks.shape, bf16), VMEM(diag_values.shape, f32)],
+                in_specs=[vmem_spec()] + [pl.BlockSpec(memory_space=HBM)] * 2,
+                out_specs=[vmem_spec()] * 2,
+                scratch_shapes=[pltpu.SemaphoreType.DMA((chunks,)), pltpu.SemaphoreType.DMA],
+                compiler_params=params(2 * MIB),
+                name="load",
+            )(in_vmem(q), in_hbm(coarse_blocks), in_hbm(diag_values))
+            weights = in_vmem(weights)
+            diag = in_vmem(diag)
+        kept = 1 if last else 3
+        total, *carry = pl.pallas_call(
+            functools.partial(mid_kernel, t == 0, before, keep, scale, middle, where),
+            out_shape=[VMEM(piece, f32)] * kept,
+            in_specs=[smem_spec()] * 2 + [vmem_spec()] * (4 + len(state)),
+            out_specs=[vmem_spec()] * kept,
             compiler_params=params(4 * MIB),
-            name="own",
-        )(tab, weights, in_vmem(q))
-        shapes = [VMEM(piece, f32)] if last else [VMEM(piece, f32)] * 3 + [VMEM(piece, bf16)]
+            name="mid",
+        )(
+            block_counts, tab, weights, in_vmem(q), in_vmem(even), diag,
+            *[in_vmem(x) for x in state],
+        )
+        shapes = [VMEM(piece, f32)] if last else [VMEM(piece, f32), VMEM(piece, bf16)]
         result = pl.pallas_call(
-            functools.partial(step_kernel, keep, scale, last, where),
+            functools.partial(step_kernel, scale, last, where),
             out_shape=shapes,
-            in_specs=[smem_spec()] * 2 + [vmem_spec()] * 8,
+            in_specs=[smem_spec()] * 2 + [vmem_spec()] * 3,
             out_specs=[vmem_spec()] * len(shapes),
             compiler_params=params(4 * MIB),
             name="step",
-        )(
-            block_counts, tab, weights, in_vmem(odd), in_vmem(even), in_vmem(own), diag,
-            in_vmem(rem), in_vmem(upd), in_vmem(sol),
-        )
+        )(block_counts, tab, weights, in_vmem(odd), in_vmem(total if last else carry[1]))
         if last:
             sol = result[0]
         else:
-            rem, upd, sol, q = result
+            late, q = result
+            state = [carry[0], carry[1], total, late]
+            before = scale
 
     parts = [sol] + [
         lax.ppermute(sol, "fine", [(a, a ^ m) for a in range(fine)]) for m in range(1, fine)

time: 40.9 us -> 40.1 us (0.980)
  Pallas kernels: 5.84 us -> 7.5 us
  local copies, waits for them, and re-layouts: 1.59 us -> 0 us
  waiting for transfers between devices: 21.8 us -> 21 us
    pallas_call x10 -> x11, Pallas kernels: 2.53 us -> 4.6 us  [the longest x5 1.98 us: body(): pl.pallas_call(functools.partial(mid_kernel, t == 0, before, keep, scale,...]
    ppermute x5, waiting for transfers between devices: 11.2 us -> 9.45 us  [body(): odd = lax.ppermute(q, ('coarse', 'fine'), odd_pairs)]
    unnamed x4 -> x0, local copies, waits for them, and re-layouts: 1.59 us -> none
    ppermute x5, waiting for transfers between devices: 8.37 us -> 9.38 us  [body(): even = lax.ppermute(q, ('coarse', 'fine'), even_pairs)]
  transfers between devices with their start and end apart: 12 -> 12, of which waited for: 11 -> 11; matrix products, arithmetic and copies ran while one was open for 0% -> 0% of each run, Pallas kernels for 3% -> 9%
where the time goes in v3:
time: 40.1 us; the launch traced here: 40 us
  waiting for transfers between devices  21 us (52%)
  starting transfers between devices  10 us (25%)
  Pallas kernels  7.5 us (19%)
  between operations  1.39 us (3%)
    ppermute x5, waiting for transfers between devices, body(): odd = lax.ppermute(q, ('coarse', 'fine'), odd_pairs)  9.45 us
    ppermute x5, waiting for transfers between devices, body(): even = lax.ppermute(q, ('coarse', 'fine'), even_pairs)  9.38 us
    ppermute x5, starting transfers between devices, body(): odd = lax.ppermute(q, ('coarse', 'fine'), odd_pairs)  5.17 us
    ppermute x5, starting transfers between devices, body(): even = lax.ppermute(q, ('coarse', 'fine'), even_pairs)  3.9 us
    pallas_call x5, Pallas kernels, body(): pl.pallas_call(functools.partial(mid_kernel, t == 0, before, keep, scale,...  1.98 us
    pallas_call x1, Pallas kernels, body(): pl.pallas_call(functools.partial(restrict_kernel, chunks, owners, fine),...  1.81 us
    pallas_call x1, Pallas kernels, body(): pl.pallas_call(functools.partial(load_kernel, chunks), out_shape=[VMEM(co...  1.57 us
    ppermute x1, waiting for transfers between devices, body(): lax.ppermute(sol, 'fine', [(a, a ^ m) for a in range(fine)])  1.2 us
  transfers between devices with their start and end apart: 12, of which 11 were waited for; matrix products, arithmetic and copies ran while one was open for 0% of the time, Pallas kernels for 9%

profile of v3, /device:TPU:9, one launch (start us, length us, event | category | flops | bytes accessed | tf_op | source)
XLA Modules:
  0.0 40.0 jit_solution(8431245341306212891)
XLA Ops:
  0.6 1.8 %restrict.1 = (bf16[32,128,128]{2,1,0:T(8,128)(2,1)S(1)}, s32[101]{0:T(128)S(4)}, f32[16,16,128]{2,1,0:T(8,128)S(1)}, f32[16,16,128]{2,1,0:T(8,128)S(1)}) custom-call(s32[32]{0:T(128)} %agg_hbm.1, s32[4,16]{1,0:T(4,128)} %bitcast.1, bf16[32,32,128]{2,1,0:T(8,128)(2,1)} %res_hbm.1, bf16[32,128,128]{2,1,0:T(8,128)(2,1)} %pro_hbm.1), custom_call_target="tpu_custom_call" | custom-call | tf_op jit(solution)/shard_map/restrict/pallas_call | solution.py:290
  2.4 0.7 %collective-permute-start = (f32[16,16,128]{2,1,0:T(8,128)S(1)}, f32[16,16,128]{2,1,0:T(8,128)S(1)}, u32[]{:S(2)}, u32[]{:S(2)}) collective-permute-start(f32[16,16,128]{2,1,0:T(8,128)S(1)} %get-tuple-element.31), channel_id=1, source_target_pairs={{0,1},{1,0},{2,3},{3,2},{4,5},{5,4},{6,7},{7,6},{8,9},{9,8},{10,11... | collective-permute-start | bytes 393224 | tf_op jit(solution)/shard_map/ppermute | solution.py:313
  3.2 1.0 %collective-permute-done = f32[16,16,128]{2,1,0:T(8,128)S(1)} collective-permute-done((f32[16,16,128]{2,1,0:T(8,128)S(1)}, f32[16,16,128]{2,1,0:T(8,128)S(1)}, u32[]{:S(2)}, u32[]{:S(2)}) %collective-permute-start) | collective-permute-done | bytes 131104 | tf_op jit(solution)/shard_map/ppermute | solution.py:313
  4.2 1.5 %collective-permute-start.2 = (bf16[16,16,128]{2,1,0:T(8,128)(2,1)S(1)}, bf16[16,16,128]{2,1,0:T(8,128)(2,1)S(1)}, u32[]{:S(2)}, u32[]{:S(2)}) collective-permute-start(bf16[16,16,128]{2,1,0:T(8,128)(2,1)S(1)} %get-tuple-element.54.after_ref.q_ref), channel_id=1, source_target_pairs={{0,3},{3,0},{1,2},{2,1},{4,7},{7,4},{5,6},{6,5},{8,11},{11,8},{9,1... | collective-permute-start | bytes 196616 | tf_op jit(solution)/shard_map/ppermute | solution.py:324
  5.7 1.1 %collective-permute-start.1 = (bf16[16,16,128]{2,1,0:T(8,128)(2,1)S(1)}, bf16[16,16,128]{2,1,0:T(8,128)(2,1)S(1)}, u32[]{:S(2)}, u32[]{:S(2)}) collective-permute-start(bf16[16,16,128]{2,1,0:T(8,128)(2,1)S(1)} %get-tuple-element.54.after_ref.q_ref), channel_id=1, source_target_pairs={{2,5},{5,2},{3,4},{4,3},{6,9},{9,6},{7,8},{8,7},{10,13},{13,10},{1... | collective-permute-start | bytes 196616 | tf_op jit(solution)/shard_map/ppermute | solution.py:323
  7.5 1.6 %load.1 = (bf16[16,4,128,128]{3,2,1,0:T(8,128)(2,1)S(1)}, f32[16,128]{1,0:T(8,128)S(1)}) custom-call(bf16[16,16,128]{2,1,0:T(8,128)(2,1)S(1)} %get-tuple-element.54.after_ref.q_ref, bf16[16,4,128,128]{3,2,1,0:T(8,128)(2,1)} %w_hbm.1, f32[16,128]{1,0:T(8,128)} %diag_hbm.1), custom_call_target="tpu_custom_call" | custom-call | tf_op jit(solution)/shard_map/load/pallas_call | solution.py:326
  9.1 0.0 collective-permute-done.2.even_ref
  9.1 0.4 mid.5
  9.5 1.9 %collective-permute-done.1.odd_ref = bf16[16,16,128]{2,1,0:T(8,128)(2,1)S(1)} collective-permute-done((bf16[16,16,128]{2,1,0:T(8,128)(2,1)S(1)}, bf16[16,16,128]{2,1,0:T(8,128)(2,1)S(1)}, u32[]{:S(2)}, u32[]{:S(2)}) %collective-permute-start.1) | collective-permute-done | bytes 65568 | tf_op jit(solution)/shard_map/ppermute | solution.py:323
  11.4 0.2 step.5
  11.6 0.8 %collective-permute-start.4 = (bf16[16,16,128]{2,1,0:T(8,128)(2,1)S(1)}, bf16[16,16,128]{2,1,0:T(8,128)(2,1)S(1)}, u32[]{:S(2)}, u32[]{:S(2)}) collective-permute-start(bf16[16,16,128]{2,1,0:T(8,128)(2,1)S(1)} %get-tuple-element.35.q_ref), channel_id=1, source_target_pairs={{0,3},{3,0},{1,2},{2,1},{4,7},{7,4},{5,6},{6,5},{8,11},{11,8},{9,1... | collective-permute-start | bytes 196616 | tf_op jit(solution)/shard_map/ppermute | solution.py:324
  12.4 0.9 %collective-permute-start.3 = (bf16[16,16,128]{2,1,0:T(8,128)(2,1)S(1)}, bf16[16,16,128]{2,1,0:T(8,128)(2,1)S(1)}, u32[]{:S(2)}, u32[]{:S(2)}) collective-permute-start(bf16[16,16,128]{2,1,0:T(8,128)(2,1)S(1)} %get-tuple-element.35.q_ref), channel_id=1, source_target_pairs={{2,5},{5,2},{3,4},{4,3},{6,9},{9,6},{7,8},{8,7},{10,13},{13,10},{1... | collective-permute-start | bytes 196616 | tf_op jit(solution)/shard_map/ppermute | solution.py:323
  13.3 2.2 %collective-permute-done.4.even_ref = bf16[16,16,128]{2,1,0:T(8,128)(2,1)S(1)} collective-permute-done((bf16[16,16,128]{2,1,0:T(8,128)(2,1)S(1)}, bf16[16,16,128]{2,1,0:T(8,128)(2,1)S(1)}, u32[]{:S(2)}, u32[]{:S(2)}) %collective-permute-start.4) | collective-permute-done | bytes 65568 | tf_op jit(solution)/shard_map/ppermute | solution.py:324
  15.5 0.4 mid.6
  15.9 2.2 %collective-permute-done.3.odd_ref = bf16[16,16,128]{2,1,0:T(8,128)(2,1)S(1)} collective-permute-done((bf16[16,16,128]{2,1,0:T(8,128)(2,1)S(1)}, bf16[16,16,128]{2,1,0:T(8,128)(2,1)S(1)}, u32[]{:S(2)}, u32[]{:S(2)}) %collective-permute-start.3) | collective-permute-done | bytes 65568 | tf_op jit(solution)/shard_map/ppermute | solution.py:323
  18.1 0.2 step.6
  18.3 0.4 collective-permute-start.6
  18.7 1.1 %collective-permute-start.5 = (bf16[16,16,128]{2,1,0:T(8,128)(2,1)S(1)}, bf16[16,16,128]{2,1,0:T(8,128)(2,1)S(1)}, u32[]{:S(2)}, u32[]{:S(2)}) collective-permute-start(bf16[16,16,128]{2,1,0:T(8,128)(2,1)S(1)} %get-tuple-element.40.q_ref), channel_id=1, source_target_pairs={{2,5},{5,2},{3,4},{4,3},{6,9},{9,6},{7,8},{8,7},{10,13},{13,10},{1... | collective-permute-start | bytes 196616 | tf_op jit(solution)/shard_map/ppermute | solution.py:323
  19.8 2.6 %collective-permute-done.6.even_ref = bf16[16,16,128]{2,1,0:T(8,128)(2,1)S(1)} collective-permute-done((bf16[16,16,128]{2,1,0:T(8,128)(2,1)S(1)}, bf16[16,16,128]{2,1,0:T(8,128)(2,1)S(1)}, u32[]{:S(2)}, u32[]{:S(2)}) %collective-permute-start.6) | collective-permute-done | bytes 65568 | tf_op jit(solution)/shard_map/ppermute | solution.py:324
  22.4 0.4 mid.7
  22.8 1.5 %collective-permute-done.5.odd_ref = bf16[16,16,128]{2,1,0:T(8,128)(2,1)S(1)} collective-permute-done((bf16[16,16,128]{2,1,0:T(8,128)(2,1)S(1)}, bf16[16,16,128]{2,1,0:T(8,128)(2,1)S(1)}, u32[]{:S(2)}, u32[]{:S(2)}) %collective-permute-start.5) | collective-permute-done | bytes 65568 | tf_op jit(solution)/shard_map/ppermute | solution.py:323
  24.3 0.2 step.7
  24.5 0.8 %collective-permute-start.8 = (bf16[16,16,128]{2,1,0:T(8,128)(2,1)S(1)}, bf16[16,16,128]{2,1,0:T(8,128)(2,1)S(1)}, u32[]{:S(2)}, u32[]{:S(2)}) collective-permute-start(bf16[16,16,128]{2,1,0:T(8,128)(2,1)S(1)} %get-tuple-element.45.q_ref), channel_id=1, source_target_pairs={{0,3},{3,0},{1,2},{2,1},{4,7},{7,4},{5,6},{6,5},{8,11},{11,8},{9,1... | collective-permute-start | bytes 196616 | tf_op jit(solution)/shard_map/ppermute | solution.py:324
  25.4 0.9 %collective-permute-start.7 = (bf16[16,16,128]{2,1,0:T(8,128)(2,1)S(1)}, bf16[16,16,128]{2,1,0:T(8,128)(2,1)S(1)}, u32[]{:S(2)}, u32[]{:S(2)}) collective-permute-start(bf16[16,16,128]{2,1,0:T(8,128)(2,1)S(1)} %get-tuple-element.45.q_ref), channel_id=1, source_target_pairs={{2,5},{5,2},{3,4},{4,3},{6,9},{9,6},{7,8},{8,7},{10,13},{13,10},{1... | collective-permute-start | bytes 196616 | tf_op jit(solution)/shard_map/ppermute | solution.py:323
  26.3 2.2 %collective-permute-done.8.even_ref = bf16[16,16,128]{2,1,0:T(8,128)(2,1)S(1)} collective-permute-done((bf16[16,16,128]{2,1,0:T(8,128)(2,1)S(1)}, bf16[16,16,128]{2,1,0:T(8,128)(2,1)S(1)}, u32[]{:S(2)}, u32[]{:S(2)}) %collective-permute-start.8) | collective-permute-done | bytes 65568 | tf_op jit(solution)/shard_map/ppermute | solution.py:324
  28.4 0.4 mid.8
  28.8 2.2 %collective-permute-done.7.odd_ref = bf16[16,16,128]{2,1,0:T(8,128)(2,1)S(1)} collective-permute-done((bf16[16,16,128]{2,1,0:T(8,128)(2,1)S(1)}, bf16[16,16,128]{2,1,0:T(8,128)(2,1)S(1)}, u32[]{:S(2)}, u32[]{:S(2)}) %collective-permute-start.7) | collective-permute-done | bytes 65568 | tf_op jit(solution)/shard_map/ppermute | solution.py:323
  31.0 0.2 step.8
  31.2 0.4 collective-permute-start.10
  31.6 1.1 %collective-permute-start.9 = (bf16[16,16,128]{2,1,0:T(8,128)(2,1)S(1)}, bf16[16,16,128]{2,1,0:T(8,128)(2,1)S(1)}, u32[]{:S(2)}, u32[]{:S(2)}) collective-permute-start(bf16[16,16,128]{2,1,0:T(8,128)(2,1)S(1)} %get-tuple-element.50.q_ref), channel_id=1, source_target_pairs={{2,5},{5,2},{3,4},{4,3},{6,9},{9,6},{7,8},{8,7},{10,13},{13,10},{1... | collective-permute-start | bytes 196616 | tf_op jit(solution)/shard_map/ppermute | solution.py:323
  32.7 2.4 %collective-permute-done.10.even_ref = bf16[16,16,128]{2,1,0:T(8,128)(2,1)S(1)} collective-permute-done((bf16[16,16,128]{2,1,0:T(8,128)(2,1)S(1)}, bf16[16,16,128]{2,1,0:T(8,128)(2,1)S(1)}, u32[]{:S(2)}, u32[]{:S(2)}) %collective-permute-start.10) | collective-permute-done | bytes 65568 | tf_op jit(solution)/shard_map/ppermute | solution.py:324
  35.1 0.4 mid.9.base_ref
  35.5 1.7 %collective-permute-done.9.odd_ref = bf16[16,16,128]{2,1,0:T(8,128)(2,1)S(1)} collective-permute-done((bf16[16,16,128]{2,1,0:T(8,128)(2,1)S(1)}, bf16[16,16,128]{2,1,0:T(8,128)(2,1)S(1)}, u32[]{:S(2)}, u32[]{:S(2)}) %collective-permute-start.9) | collective-permute-done | bytes 65568 | tf_op jit(solution)/shard_map/ppermute | solution.py:323
  37.2 0.2 step.9.rest_0_
  37.5 0.2 collective-permute-start.11
  37.7 1.2 %collective-permute-done.11.rest_1_ = f32[16,16,128]{2,1,0:T(8,128)S(1)} collective-permute-done((f32[16,16,128]{2,1,0:T(8,128)S(1)}, f32[16,16,128]{2,1,0:T(8,128)S(1)}, u32[]{:S(2)}, u32[]{:S(2)}) %collective-permute-start.11) | collective-permute-done | bytes 131104 | tf_op jit(solution)/shard_map/ppermute | solution.py:366
  38.9 1.1 %prolong.1 = (f32[32,32,128]{2,1,0:T(8,128)}, f32[16,32,128]{2,1,0:T(8,128)}) custom-call(s32[101]{0:T(128)S(4)} %get-tuple-element.28.tab_ref, bf16[32,128,128]{2,1,0:T(8,128)(2,1)S(1)} %get-tuple-element.29.pro_ref, f32[16,16,128]{2,1,0:T(8,128)S(1)} %step.9.rest_0_, f32[16,16,128]{2,1,0:T(8,128)S(1)} %collective-permute-done.11.rest_1_), custom_call_target="tpu_custom_call" | custom-call | tf_op jit(solution)/shard_map/prolong/pallas_call | solution.py:368
  (1 shorter events, 0.0 us)
Async XLA Ops:
  2.4 1.7 %collective-permute-start = (f32[16,16,128]{2,1,0:T(8,128)S(1)}, f32[16,16,128]{2,1,0:T(8,128)S(1)}, u32[]{:S(2)}, u32[]{:S(2)}) collective-permute-start(f32[16,16,128]{2,1,0:T(8,128)S(1)} %get-tuple-element.31), channel_id=1, source_target_pairs={{0,1},{1,0},{2,3},{3,2},{4,5},{5,4},{6,7},{7,6},{8,9},{9,8},{10,11... | collective-permute-start | bytes 393224 | tf_op jit(solution)/shard_map/ppermute | solution.py:313
  4.2 4.9 %collective-permute-start.2 = (bf16[16,16,128]{2,1,0:T(8,128)(2,1)S(1)}, bf16[16,16,128]{2,1,0:T(8,128)(2,1)S(1)}, u32[]{:S(2)}, u32[]{:S(2)}) collective-permute-start(bf16[16,16,128]{2,1,0:T(8,128)(2,1)S(1)} %get-tuple-element.54.after_ref.q_ref), channel_id=1, source_target_pairs={{0,3},{3,0},{1,2},{2,1},{4,7},{7,4},{5,6},{6,5},{8,11},{11,8},{9,1... | collective-permute-start | bytes 196616 | tf_op jit(solution)/shard_map/ppermute | solution.py:324
  5.7 5.6 %collective-permute-start.1 = (bf16[16,16,128]{2,1,0:T(8,128)(2,1)S(1)}, bf16[16,16,128]{2,1,0:T(8,128)(2,1)S(1)}, u32[]{:S(2)}, u32[]{:S(2)}) collective-permute-start(bf16[16,16,128]{2,1,0:T(8,128)(2,1)S(1)} %get-tuple-element.54.after_ref.q_ref), channel_id=1, source_target_pairs={{2,5},{5,2},{3,4},{4,3},{6,9},{9,6},{7,8},{8,7},{10,13},{13,10},{1... | collective-permute-start | bytes 196616 | tf_op jit(solution)/shard_map/ppermute | solution.py:323
  11.6 3.9 %collective-permute-start.4 = (bf16[16,16,128]{2,1,0:T(8,128)(2,1)S(1)}, bf16[16,16,128]{2,1,0:T(8,128)(2,1)S(1)}, u32[]{:S(2)}, u32[]{:S(2)}) collective-permute-start(bf16[16,16,128]{2,1,0:T(8,128)(2,1)S(1)} %get-tuple-element.35.q_ref), channel_id=1, source_target_pairs={{0,3},{3,0},{1,2},{2,1},{4,7},{7,4},{5,6},{6,5},{8,11},{11,8},{9,1... | collective-permute-start | bytes 196616 | tf_op jit(solution)/shard_map/ppermute | solution.py:324
  12.4 5.7 %collective-permute-start.3 = (bf16[16,16,128]{2,1,0:T(8,128)(2,1)S(1)}, bf16[16,16,128]{2,1,0:T(8,128)(2,1)S(1)}, u32[]{:S(2)}, u32[]{:S(2)}) collective-permute-start(bf16[16,16,128]{2,1,0:T(8,128)(2,1)S(1)} %get-tuple-element.35.q_ref), channel_id=1, source_target_pairs={{2,5},{5,2},{3,4},{4,3},{6,9},{9,6},{7,8},{8,7},{10,13},{13,10},{1... | collective-permute-start | bytes 196616 | tf_op jit(solution)/shard_map/ppermute | solution.py:323
  18.3 4.1 %collective-permute-start.6 = (bf16[16,16,128]{2,1,0:T(8,128)(2,1)S(1)}, bf16[16,16,128]{2,1,0:T(8,128)(2,1)S(1)}, u32[]{:S(2)}, u32[]{:S(2)}) collective-permute-start(bf16[16,16,128]{2,1,0:T(8,128)(2,1)S(1)} %get-tuple-element.40.q_ref), channel_id=1, source_target_pairs={{0,3},{3,0},{1,2},{2,1},{4,7},{7,4},{5,6},{6,5},{8,11},{11,8},{9,1... | collective-permute-start | bytes 196616 | tf_op jit(solution)/shard_map/ppermute | solution.py:324
  18.7 5.7 %collective-permute-start.5 = (bf16[16,16,128]{2,1,0:T(8,128)(2,1)S(1)}, bf16[16,16,128]{2,1,0:T(8,128)(2,1)S(1)}, u32[]{:S(2)}, u32[]{:S(2)}) collective-permute-start(bf16[16,16,128]{2,1,0:T(8,128)(2,1)S(1)} %get-tuple-element.40.q_ref), channel_id=1, source_target_pairs={{2,5},{5,2},{3,4},{4,3},{6,9},{9,6},{7,8},{8,7},{10,13},{13,10},{1... | collective-permute-start | bytes 196616 | tf_op jit(solution)/shard_map/ppermute | solution.py:323
  24.5 3.9 %collective-permute-start.8 = (bf16[16,16,128]{2,1,0:T(8,128)(2,1)S(1)}, bf16[16,16,128]{2,1,0:T(8,128)(2,1)S(1)}, u32[]{:S(2)}, u32[]{:S(2)}) collective-permute-start(bf16[16,16,128]{2,1,0:T(8,128)(2,1)S(1)} %get-tuple-element.45.q_ref), channel_id=1, source_target_pairs={{0,3},{3,0},{1,2},{2,1},{4,7},{7,4},{5,6},{6,5},{8,11},{11,8},{9,1... | collective-permute-start | bytes 196616 | tf_op jit(solution)/shard_map/ppermute | solution.py:324
  25.4 5.7 %collective-permute-start.7 = (bf16[16,16,128]{2,1,0:T(8,128)(2,1)S(1)}, bf16[16,16,128]{2,1,0:T(8,128)(2,1)S(1)}, u32[]{:S(2)}, u32[]{:S(2)}) collective-permute-start(bf16[16,16,128]{2,1,0:T(8,128)(2,1)S(1)} %get-tuple-element.45.q_ref), channel_id=1, source_target_pairs={{2,5},{5,2},{3,4},{4,3},{6,9},{9,6},{7,8},{8,7},{10,13},{13,10},{1... | collective-permute-start | bytes 196616 | tf_op jit(solution)/shard_map/ppermute | solution.py:323
  31.2 3.9 %collective-permute-start.10 = (bf16[16,16,128]{2,1,0:T(8,128)(2,1)S(1)}, bf16[16,16,128]{2,1,0:T(8,128)(2,1)S(1)}, u32[]{:S(2)}, u32[]{:S(2)}) collective-permute-start(bf16[16,16,128]{2,1,0:T(8,128)(2,1)S(1)} %get-tuple-element.50.q_ref), channel_id=1, source_target_pairs={{0,3},{3,0},{1,2},{2,1},{4,7},{7,4},{5,6},{6,5},{8,11},{11,8},{9,1... | collective-permute-start | bytes 196616 | tf_op jit(solution)/shard_map/ppermute | solution.py:324
  31.6 5.7 %collective-permute-start.9 = (bf16[16,16,128]{2,1,0:T(8,128)(2,1)S(1)}, bf16[16,16,128]{2,1,0:T(8,128)(2,1)S(1)}, u32[]{:S(2)}, u32[]{:S(2)}) collective-permute-start(bf16[16,16,128]{2,1,0:T(8,128)(2,1)S(1)} %get-tuple-element.50.q_ref), channel_id=1, source_target_pairs={{2,5},{5,2},{3,4},{4,3},{6,9},{9,6},{7,8},{8,7},{10,13},{13,10},{1... | collective-permute-start | bytes 196616 | tf_op jit(solution)/shard_map/ppermute | solution.py:323
  37.5 1.4 %collective-permute-start.11 = (f32[16,16,128]{2,1,0:T(8,128)S(1)}, f32[16,16,128]{2,1,0:T(8,128)S(1)}, u32[]{:S(2)}, u32[]{:S(2)}) collective-permute-start(f32[16,16,128]{2,1,0:T(8,128)S(1)} %step.9.rest_0_), channel_id=1, source_target_pairs={{0,1},{1,0},{2,3},{3,2},{4,5},{5,4},{6,7},{7,6},{8,9},{9,8},{10,11... | collective-permute-start | bytes 393224 | tf_op jit(solution)/shard_map/ppermute | solution.py:366

commit v4 on v3

--- a/solution.py
+++ b/solution.py
@@ -210,6 +210,37 @@
             else:
                 outs[0][b] = late
                 outs[1][b] = new.astype(outs[1].dtype)
+
+
+def share_kernel(m, chunks, where, tab_ref, pro_ref, part_ref, *rest):
+    cor_hbm, sol_hbm, rounded_ref, cor_ref, sems, sol_sem = rest[-6:]
+    share = part_ref.shape[1]
+    rows = pl.ds(pl.multiple_of((tab_ref[where["mine"]] ^ m) * share, share), share)
+    sol_copy = pltpu.make_async_copy(part_ref, sol_hbm.at[:, rows], sol_sem)
+    sol_copy.start()
+    rounded_ref[...] = part_ref[...].astype(rounded_ref.dtype)
+    blocks = pro_ref.shape[0]
+    size = blocks // chunks
+    group = 2 if size % 2 == 0 else 1
+
+    def copy(c):
+        part = pl.ds(c * size, size)
+        return pltpu.make_async_copy(cor_ref.at[part], cor_hbm.at[part, rows], sems.at[c])
+
+    for c in range(chunks):
+        for first in range(c * size, (c + 1) * size, group):
+            members = range(first, first + group)
+            both = jnp.dot(
+                on_diagonal([rounded_ref[tab_ref[where["agg"] + i]] for i in members]),
+                jnp.concatenate([pro_ref[i] for i in members], axis=0),
+                preferred_element_type=jnp.float32,
+            )
+            for j, i in enumerate(members):
+                cor_ref[i] = both[j * share : (j + 1) * share]
+        copy(c).start()
+    sol_copy.wait()
+    for c in range(chunks):
+        copy(c).wait()
 
 
 def load_kernel(chunks, after_ref, w_hbm, diag_hbm, w_ref, diag_ref, sems, diag_sem):
@@ -365,24 +396,48 @@
     parts = [sol] + [
         lax.ppermute(sol, "fine", [(a, a ^ m) for a in range(fine)]) for m in range(1, fine)
     ]
-    correction, solution = pl.pallas_call(
-        functools.partial(prolong_kernel, chunks, fine, where),
-        out_shape=[
-            HBM(fine_residual.shape, f32),
-            HBM((slots, rhs, width), f32),
-        ],
-        in_specs=[smem_spec(), vmem_spec()] + [vmem_spec()] * fine,
-        out_specs=[pl.BlockSpec(memory_space=HBM)] * 2,
-        scratch_shapes=[
-            VMEM((slots, rhs, width), f32),
-            VMEM((slots, rhs, width), bf16),
-            VMEM(fine_residual.shape, f32),
-            pltpu.SemaphoreType.DMA((chunks,)),
-            pltpu.SemaphoreType.DMA,
-        ],
-        compiler_params=params(8 * MIB),
-        name="prolong",
-    )(tab, in_vmem(pro), *[in_vmem(p) for p in parts])
+    if share % 8 == 0:
+        buffers = []
+        for m in range(fine):
+            buffers = pl.pallas_call(
+                functools.partial(share_kernel, m, chunks, where),
+                out_shape=[
+                    HBM(fine_residual.shape, f32),
+                    HBM((slots, rhs, width), f32),
+                ],
+                in_specs=[smem_spec(), vmem_spec(), vmem_spec()]
+                + [pl.BlockSpec(memory_space=HBM)] * len(buffers),
+                out_specs=[pl.BlockSpec(memory_space=HBM)] * 2,
+                scratch_shapes=[
+                    VMEM(piece, bf16),
+                    VMEM((blocks, share, width), f32),
+                    pltpu.SemaphoreType.DMA((chunks,)),
+                    pltpu.SemaphoreType.DMA,
+                ],
+                input_output_aliases={3 + i: i for i in range(len(buffers))},
+                compiler_params=params(8 * MIB),
+                name="prolong",
+            )(tab, in_vmem(pro), in_vmem(parts[m]), *[in_hbm(x) for x in buffers])
+        correction, solution = buffers
+    else:
+        correction, solution = pl.pallas_call(
+            functools.partial(prolong_kernel, chunks, fine, where),
+            out_shape=[
+                HBM(fine_residual.shape, f32),
+                HBM((slots, rhs, width), f32),
+            ],
+            in_specs=[smem_spec(), vmem_spec()] + [vmem_spec()] * fine,
+            out_specs=[pl.BlockSpec(memory_space=HBM)] * 2,
+            scratch_shapes=[
+                VMEM((slots, rhs, width), f32),
+                VMEM((slots, rhs, width), bf16),
+                VMEM(fine_residual.shape, f32),
+                pltpu.SemaphoreType.DMA((chunks,)),
+                pltpu.SemaphoreType.DMA,
+            ],
+            compiler_params=params(8 * MIB),
+            name="prolong",
+        )(tab, in_vmem(pro), *[in_vmem(p) for p in parts])
     return correction, solution
 
 

time: 40.1 us -> 40 us (level)
  waiting for transfers between devices: 21 us -> 20 us
  Pallas kernels: 7.5 us -> 8.34 us
    ppermute x1, waiting for transfers between devices: 1.2 us -> 0.25 us  [body(): lax.ppermute(sol, 'fine', [(a, a ^ m) for a in range(fine)])]
    pallas_call x1 -> x2, Pallas kernels: 1.09 us -> 1.92 us  [body(): pl.pallas_call(functools.partial(share_kernel, m, chunks, where), out_sha...]
  transfers between devices with their start and end apart: 12 -> 12, of which waited for: 11 -> 11; matrix products, arithmetic and copies ran while one was open for 0% -> 0% of each run, Pallas kernels for 9% -> 11%
where the time goes in v4:
time: 40 us; the launch traced here: 39.8 us
  waiting for transfers between devices  20 us (50%)
  starting transfers between devices  10.1 us (25%)
  Pallas kernels  8.34 us (21%)
  between operations  1.4 us (4%)
    ppermute x5, waiting for transfers between devices, body(): odd = lax.ppermute(q, ('coarse', 'fine'), odd_pairs)  9.43 us
    ppermute x5, waiting for transfers between devices, body(): even = lax.ppermute(q, ('coarse', 'fine'), even_pairs)  9.33 us
    ppermute x5, starting transfers between devices, body(): odd = lax.ppermute(q, ('coarse', 'fine'), odd_pairs)  5.22 us
    ppermute x5, starting transfers between devices, body(): even = lax.ppermute(q, ('coarse', 'fine'), even_pairs)  3.92 us
    pallas_call x5, Pallas kernels, body(): pl.pallas_call(functools.partial(mid_kernel, t == 0, before, keep, scale,...  1.98 us
    pallas_call x2, Pallas kernels, body(): pl.pallas_call(functools.partial(share_kernel, m, chunks, where), out_sha...  1.92 us
    pallas_call x1, Pallas kernels, body(): pl.pallas_call(functools.partial(restrict_kernel, chunks, owners, fine),...  1.82 us
    pallas_call x1, Pallas kernels, body(): pl.pallas_call(functools.partial(load_kernel, chunks), out_shape=[VMEM(co...  1.57 us
  transfers between devices with their start and end apart: 12, of which 11 were waited for; matrix products, arithmetic and copies ran while one was open for 0% of the time, Pallas kernels for 11%

profile of v4, /device:TPU:9, one launch (start us, length us, event | category | flops | bytes accessed | tf_op | source)
XLA Modules:
  0.0 39.8 jit_solution(8703367403562712776)
XLA Ops:
  0.6 1.8 %restrict.1 = (bf16[32,128,128]{2,1,0:T(8,128)(2,1)S(1)}, s32[101]{0:T(128)S(4)}, f32[16,16,128]{2,1,0:T(8,128)S(1)}, f32[16,16,128]{2,1,0:T(8,128)S(1)}) custom-call(s32[32]{0:T(128)} %agg_hbm.1, s32[4,16]{1,0:T(4,128)} %bitcast.1, bf16[32,32,128]{2,1,0:T(8,128)(2,1)} %res_hbm.1, bf16[32,128,128]{2,1,0:T(8,128)(2,1)} %pro_hbm.1), custom_call_target="tpu_custom_call" | custom-call | tf_op jit(solution)/shard_map/restrict/pallas_call | solution.py:321
  2.5 0.7 %collective-permute-start = (f32[16,16,128]{2,1,0:T(8,128)S(1)}, f32[16,16,128]{2,1,0:T(8,128)S(1)}, u32[]{:S(2)}, u32[]{:S(2)}) collective-permute-start(f32[16,16,128]{2,1,0:T(8,128)S(1)} %get-tuple-element.33), channel_id=1, source_target_pairs={{0,1},{1,0},{2,3},{3,2},{4,5},{5,4},{6,7},{7,6},{8,9},{9,8},{10,11... | collective-permute-start | bytes 393224 | tf_op jit(solution)/shard_map/ppermute | solution.py:344
  3.2 1.0 %collective-permute-done = f32[16,16,128]{2,1,0:T(8,128)S(1)} collective-permute-done((f32[16,16,128]{2,1,0:T(8,128)S(1)}, f32[16,16,128]{2,1,0:T(8,128)S(1)}, u32[]{:S(2)}, u32[]{:S(2)}) %collective-permute-start) | collective-permute-done | bytes 131104 | tf_op jit(solution)/shard_map/ppermute | solution.py:344
  4.2 1.5 %collective-permute-start.2 = (bf16[16,16,128]{2,1,0:T(8,128)(2,1)S(1)}, bf16[16,16,128]{2,1,0:T(8,128)(2,1)S(1)}, u32[]{:S(2)}, u32[]{:S(2)}) collective-permute-start(bf16[16,16,128]{2,1,0:T(8,128)(2,1)S(1)} %get-tuple-element.58.after_ref.q_ref), channel_id=1, source_target_pairs={{0,3},{3,0},{1,2},{2,1},{4,7},{7,4},{5,6},{6,5},{8,11},{11,8},{9,1... | collective-permute-start | bytes 196616 | tf_op jit(solution)/shard_map/ppermute | solution.py:355
  5.7 1.1 %collective-permute-start.1 = (bf16[16,16,128]{2,1,0:T(8,128)(2,1)S(1)}, bf16[16,16,128]{2,1,0:T(8,128)(2,1)S(1)}, u32[]{:S(2)}, u32[]{:S(2)}) collective-permute-start(bf16[16,16,128]{2,1,0:T(8,128)(2,1)S(1)} %get-tuple-element.58.after_ref.q_ref), channel_id=1, source_target_pairs={{2,5},{5,2},{3,4},{4,3},{6,9},{9,6},{7,8},{8,7},{10,13},{13,10},{1... | collective-permute-start | bytes 196616 | tf_op jit(solution)/shard_map/ppermute | solution.py:354
  7.5 1.6 %load.1 = (bf16[16,4,128,128]{3,2,1,0:T(8,128)(2,1)S(1)}, f32[16,128]{1,0:T(8,128)S(1)}) custom-call(bf16[16,16,128]{2,1,0:T(8,128)(2,1)S(1)} %get-tuple-element.58.after_ref.q_ref, bf16[16,4,128,128]{3,2,1,0:T(8,128)(2,1)} %w_hbm.1, f32[16,128]{1,0:T(8,128)} %diag_hbm.1), custom_call_target="tpu_custom_call" | custom-call | tf_op jit(solution)/shard_map/load/pallas_call | solution.py:357
  9.1 0.0 collective-permute-done.2.even_ref
  9.1 0.4 mid.5
  9.5 1.9 %collective-permute-done.1.odd_ref = bf16[16,16,128]{2,1,0:T(8,128)(2,1)S(1)} collective-permute-done((bf16[16,16,128]{2,1,0:T(8,128)(2,1)S(1)}, bf16[16,16,128]{2,1,0:T(8,128)(2,1)S(1)}, u32[]{:S(2)}, u32[]{:S(2)}) %collective-permute-start.1) | collective-permute-done | bytes 65568 | tf_op jit(solution)/shard_map/ppermute | solution.py:354
  11.4 0.2 step.5
  11.6 0.8 %collective-permute-start.4 = (bf16[16,16,128]{2,1,0:T(8,128)(2,1)S(1)}, bf16[16,16,128]{2,1,0:T(8,128)(2,1)S(1)}, u32[]{:S(2)}, u32[]{:S(2)}) collective-permute-start(bf16[16,16,128]{2,1,0:T(8,128)(2,1)S(1)} %get-tuple-element.37.q_ref), channel_id=1, source_target_pairs={{0,3},{3,0},{1,2},{2,1},{4,7},{7,4},{5,6},{6,5},{8,11},{11,8},{9,1... | collective-permute-start | bytes 196616 | tf_op jit(solution)/shard_map/ppermute | solution.py:355
  12.4 0.9 %collective-permute-start.3 = (bf16[16,16,128]{2,1,0:T(8,128)(2,1)S(1)}, bf16[16,16,128]{2,1,0:T(8,128)(2,1)S(1)}, u32[]{:S(2)}, u32[]{:S(2)}) collective-permute-start(bf16[16,16,128]{2,1,0:T(8,128)(2,1)S(1)} %get-tuple-element.37.q_ref), channel_id=1, source_target_pairs={{2,5},{5,2},{3,4},{4,3},{6,9},{9,6},{7,8},{8,7},{10,13},{13,10},{1... | collective-permute-start | bytes 196616 | tf_op jit(solution)/shard_map/ppermute | solution.py:354
  13.4 2.2 %collective-permute-done.4.even_ref = bf16[16,16,128]{2,1,0:T(8,128)(2,1)S(1)} collective-permute-done((bf16[16,16,128]{2,1,0:T(8,128)(2,1)S(1)}, bf16[16,16,128]{2,1,0:T(8,128)(2,1)S(1)}, u32[]{:S(2)}, u32[]{:S(2)}) %collective-permute-start.4) | collective-permute-done | bytes 65568 | tf_op jit(solution)/shard_map/ppermute | solution.py:355
  15.5 0.4 mid.6
  15.9 2.2 %collective-permute-done.3.odd_ref = bf16[16,16,128]{2,1,0:T(8,128)(2,1)S(1)} collective-permute-done((bf16[16,16,128]{2,1,0:T(8,128)(2,1)S(1)}, bf16[16,16,128]{2,1,0:T(8,128)(2,1)S(1)}, u32[]{:S(2)}, u32[]{:S(2)}) %collective-permute-start.3) | collective-permute-done | bytes 65568 | tf_op jit(solution)/shard_map/ppermute | solution.py:354
  18.1 0.2 step.6
  18.3 0.4 collective-permute-start.6
  18.7 1.1 %collective-permute-start.5 = (bf16[16,16,128]{2,1,0:T(8,128)(2,1)S(1)}, bf16[16,16,128]{2,1,0:T(8,128)(2,1)S(1)}, u32[]{:S(2)}, u32[]{:S(2)}) collective-permute-start(bf16[16,16,128]{2,1,0:T(8,128)(2,1)S(1)} %get-tuple-element.42.q_ref), channel_id=1, source_target_pairs={{2,5},{5,2},{3,4},{4,3},{6,9},{9,6},{7,8},{8,7},{10,13},{13,10},{1... | collective-permute-start | bytes 196616 | tf_op jit(solution)/shard_map/ppermute | solution.py:354
  19.8 2.6 %collective-permute-done.6.even_ref = bf16[16,16,128]{2,1,0:T(8,128)(2,1)S(1)} collective-permute-done((bf16[16,16,128]{2,1,0:T(8,128)(2,1)S(1)}, bf16[16,16,128]{2,1,0:T(8,128)(2,1)S(1)}, u32[]{:S(2)}, u32[]{:S(2)}) %collective-permute-start.6) | collective-permute-done | bytes 65568 | tf_op jit(solution)/shard_map/ppermute | solution.py:355
  22.4 0.4 mid.7
  22.8 1.5 %collective-permute-done.5.odd_ref = bf16[16,16,128]{2,1,0:T(8,128)(2,1)S(1)} collective-permute-done((bf16[16,16,128]{2,1,0:T(8,128)(2,1)S(1)}, bf16[16,16,128]{2,1,0:T(8,128)(2,1)S(1)}, u32[]{:S(2)}, u32[]{:S(2)}) %collective-permute-start.5) | collective-permute-done | bytes 65568 | tf_op jit(solution)/shard_map/ppermute | solution.py:354
  24.3 0.2 step.7
  24.5 0.8 %collective-permute-start.8 = (bf16[16,16,128]{2,1,0:T(8,128)(2,1)S(1)}, bf16[16,16,128]{2,1,0:T(8,128)(2,1)S(1)}, u32[]{:S(2)}, u32[]{:S(2)}) collective-permute-start(bf16[16,16,128]{2,1,0:T(8,128)(2,1)S(1)} %get-tuple-element.47.q_ref), channel_id=1, source_target_pairs={{0,3},{3,0},{1,2},{2,1},{4,7},{7,4},{5,6},{6,5},{8,11},{11,8},{9,1... | collective-permute-start | bytes 196616 | tf_op jit(solution)/shard_map/ppermute | solution.py:355
  25.4 0.9 %collective-permute-start.7 = (bf16[16,16,128]{2,1,0:T(8,128)(2,1)S(1)}, bf16[16,16,128]{2,1,0:T(8,128)(2,1)S(1)}, u32[]{:S(2)}, u32[]{:S(2)}) collective-permute-start(bf16[16,16,128]{2,1,0:T(8,128)(2,1)S(1)} %get-tuple-element.47.q_ref), channel_id=1, source_target_pairs={{2,5},{5,2},{3,4},{4,3},{6,9},{9,6},{7,8},{8,7},{10,13},{13,10},{1... | collective-permute-start | bytes 196616 | tf_op jit(solution)/shard_map/ppermute | solution.py:354
  26.3 2.2 %collective-permute-done.8.even_ref = bf16[16,16,128]{2,1,0:T(8,128)(2,1)S(1)} collective-permute-done((bf16[16,16,128]{2,1,0:T(8,128)(2,1)S(1)}, bf16[16,16,128]{2,1,0:T(8,128)(2,1)S(1)}, u32[]{:S(2)}, u32[]{:S(2)}) %collective-permute-start.8) | collective-permute-done | bytes 65568 | tf_op jit(solution)/shard_map/ppermute | solution.py:355
  28.4 0.4 mid.8
  28.8 2.2 %collective-permute-done.7.odd_ref = bf16[16,16,128]{2,1,0:T(8,128)(2,1)S(1)} collective-permute-done((bf16[16,16,128]{2,1,0:T(8,128)(2,1)S(1)}, bf16[16,16,128]{2,1,0:T(8,128)(2,1)S(1)}, u32[]{:S(2)}, u32[]{:S(2)}) %collective-permute-start.7) | collective-permute-done | bytes 65568 | tf_op jit(solution)/shard_map/ppermute | solution.py:354
  31.0 0.2 step.8
  31.2 0.4 collective-permute-start.10
  31.6 1.1 %collective-permute-start.9 = (bf16[16,16,128]{2,1,0:T(8,128)(2,1)S(1)}, bf16[16,16,128]{2,1,0:T(8,128)(2,1)S(1)}, u32[]{:S(2)}, u32[]{:S(2)}) collective-permute-start(bf16[16,16,128]{2,1,0:T(8,128)(2,1)S(1)} %get-tuple-element.52.q_ref), channel_id=1, source_target_pairs={{2,5},{5,2},{3,4},{4,3},{6,9},{9,6},{7,8},{8,7},{10,13},{13,10},{1... | collective-permute-start | bytes 196616 | tf_op jit(solution)/shard_map/ppermute | solution.py:354
  32.7 2.4 %collective-permute-done.10.even_ref = bf16[16,16,128]{2,1,0:T(8,128)(2,1)S(1)} collective-permute-done((bf16[16,16,128]{2,1,0:T(8,128)(2,1)S(1)}, bf16[16,16,128]{2,1,0:T(8,128)(2,1)S(1)}, u32[]{:S(2)}, u32[]{:S(2)}) %collective-permute-start.10) | collective-permute-done | bytes 65568 | tf_op jit(solution)/shard_map/ppermute | solution.py:355
  35.2 0.4 mid.9.base_ref
  35.6 1.7 %collective-permute-done.9.odd_ref = bf16[16,16,128]{2,1,0:T(8,128)(2,1)S(1)} collective-permute-done((bf16[16,16,128]{2,1,0:T(8,128)(2,1)S(1)}, bf16[16,16,128]{2,1,0:T(8,128)(2,1)S(1)}, u32[]{:S(2)}, u32[]{:S(2)}) %collective-permute-start.9) | collective-permute-done | bytes 65568 | tf_op jit(solution)/shard_map/ppermute | solution.py:354
  37.2 0.2 step.9.part_ref
  37.4 0.2 collective-permute-start.11
  37.6 1.0 %prolong.2 = (f32[32,32,128]{2,1,0:T(8,128)}, f32[16,32,128]{2,1,0:T(8,128)}) custom-call(s32[101]{0:T(128)S(4)} %get-tuple-element.30.tab_ref, bf16[32,128,128]{2,1,0:T(8,128)(2,1)S(1)} %get-tuple-element.31.pro_ref, f32[16,16,128]{2,1,0:T(8,128)S(1)} %step.9.part_ref), custom_call_target="tpu_custom_call" | custom-call | tf_op jit(solution)/shard_map/prolong/pallas_call | solution.py:402
  38.6 0.2 collective-permute-done.11.part_ref
  38.9 1.0 %prolong.3 = (f32[32,32,128]{2,1,0:T(8,128)}, f32[16,32,128]{2,1,0:T(8,128)}) custom-call(s32[101]{0:T(128)S(4)} %get-tuple-element.30.tab_ref, bf16[32,128,128]{2,1,0:T(8,128)(2,1)S(1)} %get-tuple-element.31.pro_ref, f32[16,16,128]{2,1,0:T(8,128)S(1)} %collective-permute-done.11.part_ref, ...), custom_call_target="tpu_custom_call", output_to_operand_aliasing={{0}: (3, {}), {1}: (4, {})} | custom-call | tf_op jit(solution)/shard_map/prolong/pallas_call | solution.py:402
  (1 shorter events, 0.0 us)
Async XLA Ops:
  2.5 1.7 %collective-permute-start = (f32[16,16,128]{2,1,0:T(8,128)S(1)}, f32[16,16,128]{2,1,0:T(8,128)S(1)}, u32[]{:S(2)}, u32[]{:S(2)}) collective-permute-start(f32[16,16,128]{2,1,0:T(8,128)S(1)} %get-tuple-element.33), channel_id=1, source_target_pairs={{0,1},{1,0},{2,3},{3,2},{4,5},{5,4},{6,7},{7,6},{8,9},{9,8},{10,11... | collective-permute-start | bytes 393224 | tf_op jit(solution)/shard_map/ppermute | solution.py:344
  4.2 4.9 %collective-permute-start.2 = (bf16[16,16,128]{2,1,0:T(8,128)(2,1)S(1)}, bf16[16,16,128]{2,1,0:T(8,128)(2,1)S(1)}, u32[]{:S(2)}, u32[]{:S(2)}) collective-permute-start(bf16[16,16,128]{2,1,0:T(8,128)(2,1)S(1)} %get-tuple-element.58.after_ref.q_ref), channel_id=1, source_target_pairs={{0,3},{3,0},{1,2},{2,1},{4,7},{7,4},{5,6},{6,5},{8,11},{11,8},{9,1... | collective-permute-start | bytes 196616 | tf_op jit(solution)/shard_map/ppermute | solution.py:355
  5.7 5.6 %collective-permute-start.1 = (bf16[16,16,128]{2,1,0:T(8,128)(2,1)S(1)}, bf16[16,16,128]{2,1,0:T(8,128)(2,1)S(1)}, u32[]{:S(2)}, u32[]{:S(2)}) collective-permute-start(bf16[16,16,128]{2,1,0:T(8,128)(2,1)S(1)} %get-tuple-element.58.after_ref.q_ref), channel_id=1, source_target_pairs={{2,5},{5,2},{3,4},{4,3},{6,9},{9,6},{7,8},{8,7},{10,13},{13,10},{1... | collective-permute-start | bytes 196616 | tf_op jit(solution)/shard_map/ppermute | solution.py:354
  11.6 3.9 %collective-permute-start.4 = (bf16[16,16,128]{2,1,0:T(8,128)(2,1)S(1)}, bf16[16,16,128]{2,1,0:T(8,128)(2,1)S(1)}, u32[]{:S(2)}, u32[]{:S(2)}) collective-permute-start(bf16[16,16,128]{2,1,0:T(8,128)(2,1)S(1)} %get-tuple-element.37.q_ref), channel_id=1, source_target_pairs={{0,3},{3,0},{1,2},{2,1},{4,7},{7,4},{5,6},{6,5},{8,11},{11,8},{9,1... | collective-permute-start | bytes 196616 | tf_op jit(solution)/shard_map/ppermute | solution.py:355
  12.4 5.7 %collective-permute-start.3 = (bf16[16,16,128]{2,1,0:T(8,128)(2,1)S(1)}, bf16[16,16,128]{2,1,0:T(8,128)(2,1)S(1)}, u32[]{:S(2)}, u32[]{:S(2)}) collective-permute-start(bf16[16,16,128]{2,1,0:T(8,128)(2,1)S(1)} %get-tuple-element.37.q_ref), channel_id=1, source_target_pairs={{2,5},{5,2},{3,4},{4,3},{6,9},{9,6},{7,8},{8,7},{10,13},{13,10},{1... | collective-permute-start | bytes 196616 | tf_op jit(solution)/shard_map/ppermute | solution.py:354
  18.3 4.1 %collective-permute-start.6 = (bf16[16,16,128]{2,1,0:T(8,128)(2,1)S(1)}, bf16[16,16,128]{2,1,0:T(8,128)(2,1)S(1)}, u32[]{:S(2)}, u32[]{:S(2)}) collective-permute-start(bf16[16,16,128]{2,1,0:T(8,128)(2,1)S(1)} %get-tuple-element.42.q_ref), channel_id=1, source_target_pairs={{0,3},{3,0},{1,2},{2,1},{4,7},{7,4},{5,6},{6,5},{8,11},{11,8},{9,1... | collective-permute-start | bytes 196616 | tf_op jit(solution)/shard_map/ppermute | solution.py:355
  18.7 5.6 %collective-permute-start.5 = (bf16[16,16,128]{2,1,0:T(8,128)(2,1)S(1)}, bf16[16,16,128]{2,1,0:T(8,128)(2,1)S(1)}, u32[]{:S(2)}, u32[]{:S(2)}) collective-permute-start(bf16[16,16,128]{2,1,0:T(8,128)(2,1)S(1)} %get-tuple-element.42.q_ref), channel_id=1, source_target_pairs={{2,5},{5,2},{3,4},{4,3},{6,9},{9,6},{7,8},{8,7},{10,13},{13,10},{1... | collective-permute-start | bytes 196616 | tf_op jit(solution)/shard_map/ppermute | solution.py:354
  24.5 3.9 %collective-permute-start.8 = (bf16[16,16,128]{2,1,0:T(8,128)(2,1)S(1)}, bf16[16,16,128]{2,1,0:T(8,128)(2,1)S(1)}, u32[]{:S(2)}, u32[]{:S(2)}) collective-permute-start(bf16[16,16,128]{2,1,0:T(8,128)(2,1)S(1)} %get-tuple-element.47.q_ref), channel_id=1, source_target_pairs={{0,3},{3,0},{1,2},{2,1},{4,7},{7,4},{5,6},{6,5},{8,11},{11,8},{9,1... | collective-permute-start | bytes 196616 | tf_op jit(solution)/shard_map/ppermute | solution.py:355
  25.4 5.7 %collective-permute-start.7 = (bf16[16,16,128]{2,1,0:T(8,128)(2,1)S(1)}, bf16[16,16,128]{2,1,0:T(8,128)(2,1)S(1)}, u32[]{:S(2)}, u32[]{:S(2)}) collective-permute-start(bf16[16,16,128]{2,1,0:T(8,128)(2,1)S(1)} %get-tuple-element.47.q_ref), channel_id=1, source_target_pairs={{2,5},{5,2},{3,4},{4,3},{6,9},{9,6},{7,8},{8,7},{10,13},{13,10},{1... | collective-permute-start | bytes 196616 | tf_op jit(solution)/shard_map/ppermute | solution.py:354
  31.2 3.9 %collective-permute-start.10 = (bf16[16,16,128]{2,1,0:T(8,128)(2,1)S(1)}, bf16[16,16,128]{2,1,0:T(8,128)(2,1)S(1)}, u32[]{:S(2)}, u32[]{:S(2)}) collective-permute-start(bf16[16,16,128]{2,1,0:T(8,128)(2,1)S(1)} %get-tuple-element.52.q_ref), channel_id=1, source_target_pairs={{0,3},{3,0},{1,2},{2,1},{4,7},{7,4},{5,6},{6,5},{8,11},{11,8},{9,1... | collective-permute-start | bytes 196616 | tf_op jit(solution)/shard_map/ppermute | solution.py:355
  31.6 5.6 %collective-permute-start.9 = (bf16[16,16,128]{2,1,0:T(8,128)(2,1)S(1)}, bf16[16,16,128]{2,1,0:T(8,128)(2,1)S(1)}, u32[]{:S(2)}, u32[]{:S(2)}) collective-permute-start(bf16[16,16,128]{2,1,0:T(8,128)(2,1)S(1)} %get-tuple-element.52.q_ref), channel_id=1, source_target_pairs={{2,5},{5,2},{3,4},{4,3},{6,9},{9,6},{7,8},{8,7},{10,13},{13,10},{1... | collective-permute-start | bytes 196616 | tf_op jit(solution)/shard_map/ppermute | solution.py:354
  37.4 1.4 %collective-permute-start.11 = (f32[16,16,128]{2,1,0:T(8,128)S(1)}, f32[16,16,128]{2,1,0:T(8,128)S(1)}, u32[]{:S(2)}, u32[]{:S(2)}) collective-permute-start(f32[16,16,128]{2,1,0:T(8,128)S(1)} %step.9.part_ref), channel_id=1, source_target_pairs={{0,1},{1,0},{2,3},{3,2},{4,5},{5,4},{6,7},{7,6},{8,9},{9,8},{10,11... | collective-permute-start | bytes 393224 | tf_op jit(solution)/shard_map/ppermute | solution.py:397
